TPU v7x, 128 devices: a whole 4x4x4 slice. The times are simulated.
128 devices in a mesh: gx: 16 (over x, y), gy: 4 (over z_hi, core), gz: 2 (over z_lo).
Axes of the slice: x: 4, y: 4, z: 4 (z_hi: 2, z_lo: 2; z = z_hi * 2 + z_lo), core: 2. Of those that a mesh axis runs over, the one named last changes fastest.
Arguments:
- right_side: float32 [256, 256, 1024], P('gx', 'gy', 'gz'), may hold values from -24 to 24
- reaction: float32 [256, 256, 1024], P('gx', 'gy', 'gz'), may hold values from 0.5 to 2
- velocity: float32 [3, 256, 256, 1024], P(None, 'gx', 'gy', 'gz'), may hold values from -0.5 to 0.5
Outputs:
- solution: float32 [256, 256, 1024], P('gx', 'gy', 'gz')
- residual: float32 [256, 256, 1024], P('gx', 'gy', 'gz')
- residual_norm: float32 [], replicated
All inputs are finite; a program needn't handle non-finite values.
Results may differ from a plain program's by a relative error of at most 0.00002.
Values sent between devices are 32-bit elements; how exact they have to be, the bound alone decides.
No kernel may reach another device: no remote copies, remote signals or barrier semaphores. Data moves between devices by JAX's collectives and lax.ppermute only.
A program may use at most 128 MiB of HBM per device.

v0:
```python
import functools

import jax
import jax.numpy as jnp
from jax import lax
from jax.experimental import pallas as pl
from jax.experimental.pallas import tpu as pltpu
from jax.sharding import PartitionSpec as P


ITERS = 5
LANES = 128
COST = 10**8

centre = 7.25
half_width = 6.75


def chebyshev_weights(count):
    ratio_value = centre / half_width
    weights = [1.0 / ratio_value]
    for _ in range(count):
        weights.append(1.0 / (2.0 * ratio_value - weights[-1]))
    return weights


def step_factors(iteration):
    weights = chebyshev_weights(ITERS)
    return weights[iteration + 1] * weights[iteration], 2.0 * weights[iteration + 1] / half_width


def in_vmem(shape):
    return pltpu.VMEM(shape, jnp.float32)


def call(body, out_shape, args, spaces, out_spaces, aliases=None, scratch=(), flops=0, limit=4, nbytes=0):
    spec = {
        "v": pl.BlockSpec(memory_space=pltpu.VMEM),
        "s": pl.BlockSpec(memory_space=pltpu.SMEM),
        "h": pl.BlockSpec(memory_space=pl.ANY),
    }
    args = [
        arg if space == "s" else pltpu.with_memory_space_constraint(arg, pltpu.VMEM if space == "v" else pltpu.HBM)
        for arg, space in zip(args, spaces)
    ]
    return pl.pallas_call(
        body,
        out_shape=out_shape,
        in_specs=[spec[space] for space in spaces],
        out_specs=[spec[space] for space in out_spaces],
        input_output_aliases=aliases or {},
        scratch_shapes=list(scratch),
        compiler_params=pltpu.CompilerParams(vmem_limit_bytes=limit * 1024 * 1024),
        cost_estimate=pl.CostEstimate(flops=flops, bytes_accessed=nbytes, transcendentals=0),
    )(*args)


def position():
    me_y, last_y = lax.axis_index("gy"), lax.axis_size("gy") - 1
    inside = jnp.where((me_y > 0) & (me_y < last_y), 1, 0)
    return lax.rem(lax.axis_index("gx"), 2), lax.rem(me_y, 2), inside, lax.axis_index("gz")


def tile_iota(dim):
    return lax.broadcasted_iota(jnp.int32, (8, LANES), dim)


def column_tile(place):
    high = place[3] == 0
    offset = pl.multiple_of(jnp.where(high, 512 - LANES, 0), LANES)
    return offset, jnp.where(high, LANES - 1, 0)


def pack_columns(read, offset, lane, out_ref):
    lanes = tile_iota(1)
    parts = []
    for t in range(8):
        columns = jnp.zeros((8, LANES), jnp.float32)
        for i in range(16):
            moved = pltpu.roll(read(i, t, offset), (16 * t + i - lane) & (LANES - 1), 1)
            columns = jnp.where(lanes == 16 * t + i, moved, columns)
        parts.append(columns)
    while len(parts) > 1:
        parts = [one + other for one, other in zip(parts[::2], parts[1::2])]
    out_ref[...] = parts[0]


def sides(place):
    even_x = place[0] == 0
    even_y = place[1] == 0
    planes = jnp.where(even_x, 15, 0), jnp.where(even_x, 0, 15)
    rows = jnp.where(even_y, 63, 0), jnp.where(even_y, 0, 63)
    tiles = [pl.multiple_of(jnp.where(even_y, high, low), 8) for high, low in ((56, 0), (0, 56))]
    return planes, rows, tiles


def write_side_faces(rows_at, tile_at, place, ya, yb, zface):
    for n, face in enumerate((ya, yb)):
        values = [rows_at(n, i) for i in range(16)]
        for i in range(16):
            face[i : i + 1, :] = values[i]
    offset, lane = column_tile(place)
    pack_columns(lambda i, t, off: tile_at(i, t), offset, lane, zface)


FACES = [(64, 512), (64, 512), (16, 512), (16, 512), (8, LANES)]


def first_faces(rhs_hbm, xa, xb, ya, yb, zface, rows_a, rows_b, column, sem):
    place = position()
    planes, rows, tiles = sides(place)
    offset, _ = column_tile(place)
    copies = [
        pltpu.make_async_copy(rhs_hbm.at[:, :, pl.ds(offset, LANES)], column, sem.at[0]),
        pltpu.make_async_copy(rhs_hbm.at[:, pl.ds(tiles[0], 8), :], rows_a, sem.at[1]),
        pltpu.make_async_copy(rhs_hbm.at[:, pl.ds(tiles[1], 8), :], rows_b, sem.at[2]),
        pltpu.make_async_copy(rhs_hbm.at[planes[0]], xa, sem.at[3]),
        pltpu.make_async_copy(rhs_hbm.at[planes[1]], xb, sem.at[4]),
    ]
    for copy in copies:
        copy.start()
    for copy in copies[:3]:
        copy.wait()
    held = rows_a, rows_b
    write_side_faces(
        lambda n, i: held[n][i, pl.ds(lax.rem(rows[n], 8), 1), :],
        lambda i, t: column[i, 8 * t : 8 * t + 8, :],
        place, ya, yb, zface,
    )
    for copy in copies[3:]:
        copy.wait()


def row_of_tiles(ref, i, t):
    return [ref[i, 8 * t : 8 * t + 8, LANES * j : LANES * j + LANES] for j in range(4)]


def plane_terms(values_ref, diagonal, velocity_ref, i, emit):
    row, lane = tile_iota(0), tile_iota(1)
    first_row, last_row, first_lane, last_lane = row == 0, row == 7, lane == 0, lane == LANES - 1
    zero = jnp.zeros((8, LANES), jnp.float32)
    below = [zero] * 4
    here = row_of_tiles(values_ref, i, 0)
    for t in range(8):
        rows = slice(8 * t, 8 * t + 8)
        above = row_of_tiles(values_ref, i, t + 1) if t < 7 else [zero] * 4
        for j in range(4):
            lanes = slice(LANES * j, LANES * j + LANES)
            plus_y = pltpu.roll(jnp.where(first_row, above[j], here[j]), 7, 0)
            minus_y = pltpu.roll(jnp.where(last_row, below[j], here[j]), 1, 0)
            plus_z = pltpu.roll(jnp.where(first_lane, here[j + 1] if j < 3 else zero, here[j]), LANES - 1, 1)
            minus_z = pltpu.roll(jnp.where(last_lane, here[j - 1] if j > 0 else zero, here[j]), 1, 1)
            vx = velocity_ref[0, i, rows, lanes]
            if i == 0:
                plus_x = values_ref[i + 1, rows, lanes]
                beside = plus_x - vx * plus_x
            elif i == 15:
                minus_x = values_ref[i - 1, rows, lanes]
                beside = minus_x + vx * minus_x
            else:
                plus_x = values_ref[i + 1, rows, lanes]
                minus_x = values_ref[i - 1, rows, lanes]
                beside = plus_x - vx * (plus_x - minus_x) + minus_x
            beside = beside + (plus_y - velocity_ref[1, i, rows, lanes] * (plus_y - minus_y)) + minus_y
            beside = beside + (plus_z - velocity_ref[2, i, rows, lanes] * (plus_z - minus_z)) + minus_z
            emit(i, rows, lanes, here[j], diagonal(i, rows, lanes) * here[j] - beside)
        below, here = here, above


def first_main(rhs_ref, reaction_ref, velocity_ref, r_ref, d_ref, diag_ref, xa_c, xb_c, ya_c, yb_c, z_c):
    place = position()
    factor, gain = step_factors(0)

    def diagonal(i, rows, lanes):
        value = 6.0 + reaction_ref[i, rows, lanes]
        diag_ref[i, rows, lanes] = value
        return value

    def emit(i, rows, lanes, here, applied):
        residual = here - applied * (1.0 / centre)
        r_ref[i, rows, lanes] = residual
        d_ref[i, rows, lanes] = (factor / centre) * here + gain * residual

    for i in range(16):
        plane_terms(rhs_ref, diagonal, velocity_ref, i, emit)
    planes, _, tiles = sides(place)
    sign_x = jnp.where(place[0] == 0, -1.0, 1.0)
    sign_y = jnp.where(place[1] == 0, -1.0, 1.0)
    inside = (place[2] > 0).astype(jnp.float32)
    row = lax.broadcasted_iota(jnp.int32, (8, 512), 0)
    xa_c[...] = 1.0 + sign_x * velocity_ref[0, planes[0]]
    xb_c[...] = 1.0 - sign_x * velocity_ref[0, planes[1]]
    row_a = jnp.where(place[1] == 0, 7, 0)
    for i in range(16):
        own_a = 1.0 + sign_y * velocity_ref[1, i, pl.ds(tiles[0], 8), :]
        own_b = (1.0 - sign_y * velocity_ref[1, i, pl.ds(tiles[1], 8), :]) * inside
        ya_c[i] = jnp.where(row == row_a, own_a, 0.0)
        yb_c[i] = jnp.where(row == 7 - row_a, own_b, 0.0)
    offset, lane = column_tile(place)
    sign = jnp.where(place[3] == 0, -1.0, 1.0)
    pack_columns(
        lambda i, t, off: 1.0 + sign * velocity_ref[2, i, 8 * t : 8 * t + 8, pl.ds(off, LANES)], offset, lane, z_c
    )


def held(ref):
    return lambda i, rows, lanes: ref[i, rows, lanes]


def main(factor, gain, s_scale, d_ref, r_ref, s_ref, diag_ref, velocity_ref, r_out, d_out, s_out):
    def emit(i, rows, lanes, here, applied):
        residual = r_ref[i, rows, lanes] - applied
        r_out[i, rows, lanes] = residual
        before = s_ref[i, rows, lanes]
        s_out[i, rows, lanes] = (before if s_scale is None else before * s_scale) + here
        d_out[i, rows, lanes] = factor * here + gain * residual

    for i in range(16):
        plane_terms(d_ref, held(diag_ref), velocity_ref, i, emit)


def last_main(d_ref, r_ref, s_ref, diag_ref, velocity_ref, r_out, s_out):
    def emit(i, rows, lanes, here, applied):
        r_out[i, rows, lanes] = r_ref[i, rows, lanes] - applied
        s_out[i, rows, lanes] = s_ref[i, rows, lanes] + here

    for i in range(16):
        plane_terms(d_ref, held(diag_ref), velocity_ref, i, emit)


def correct(gain, place, scale, halos, coefs, r_ref, d_ref, ends, inner):
    hxa, hxb, hya, hyb, hz = halos
    xa_c, xb_c, ya_c, yb_c, z_c = coefs
    planes, _, tiles = sides(place)
    which = ([0, 15] if ends else []) + (list(range(1, 15)) if inner else [])

    def term(coef, halo):
        return coef * halo if scale is None else coef * halo * scale

    def add(places, changes):
        new_r = [r_ref[at] + change for at, change in zip(places, changes)]
        if d_ref is not None:
            new_d = [d_ref[at] + gain * change for at, change in zip(places, changes)]
        for n, at in enumerate(places):
            r_ref[at] = new_r[n]
            if d_ref is not None:
                d_ref[at] = new_d[n]

    if ends:
        for t in range(0, 64, 16):
            rows = slice(t, t + 16)
            add([(planes[0], rows)], [term(xa_c[rows, :], hxa[rows, :])])
            add([(planes[1], rows)], [term(xb_c[rows, :], hxb[rows, :])])
    for first in range(0, len(which), 4):
        group = which[first : first + 4]
        for tile, coef, halo in ((tiles[0], ya_c, hya), (tiles[1], yb_c, hyb)):
            changes = [term(coef[i], jnp.broadcast_to(halo[i : i + 1, :], (8, 512))) for i in group]
            add([(i, pl.ds(tile, 8)) for i in group], changes)
    offset, lane = column_tile(place)
    lanes = tile_iota(1)
    packed = term(z_c[...], hz[...])
    for t in range(8):
        rows = slice(8 * t, 8 * t + 8)
        shifts = [(lane - i - 16 * t) & (LANES - 1) for i in which]
        moved = [jnp.where(lanes == lane, pltpu.roll(packed, shift, 1), 0.0) for shift in shifts]
        add([(i, rows, pl.ds(offset, LANES)) for i in which], moved)


def fix_ends(gain, scale, *refs):
    halos, coefs, (_, _), (r_ref, d_ref, xa, xb) = refs[:5], refs[5:10], refs[10:12], refs[12:]
    place = position()
    correct(gain, place, scale, halos, coefs, r_ref, d_ref, True, False)
    planes, _, _ = sides(place)
    xa[...] = d_ref[planes[0]]
    xb[...] = d_ref[planes[1]]


def fix_inner(gain, scale, *refs):
    (hya, hyb, hz), (ya_c, yb_c, z_c), (_, _), (r_ref, d_ref, ya, yb, zface) = refs[:3], refs[3:6], refs[6:8], refs[8:]
    place = position()
    halos, coefs = (None, None, hya, hyb, hz), (None, None, ya_c, yb_c, z_c)
    correct(gain, place, scale, halos, coefs, r_ref, d_ref, False, True)
    _, rows, _ = sides(place)
    offset, _ = column_tile(place)
    write_side_faces(
        lambda n, i: d_ref[i, pl.ds(rows[n], 1), :],
        lambda i, t: d_ref[i, 8 * t : 8 * t + 8, pl.ds(offset, LANES)],
        place, ya, yb, zface,
    )


def last_fix(*refs):
    halos, coefs = refs[:5], refs[5:10]
    _, r_ref, part_ref = refs[10:]
    correct(None, position(), None, halos, coefs, r_ref, None, True, True)

    def plane(i, total):
        for t in range(8):
            value = r_ref[i, 8 * t : 8 * t + 8, :]
            total = total + value * value
        return total

    total = lax.fori_loop(0, 16, plane, jnp.zeros((8, 512), jnp.float32), unroll=2)
    part_ref[...] = jnp.broadcast_to(jnp.sum(total).reshape(1, 1), part_ref.shape)


def save(held_ref, out_hbm, sem):
    copy = pltpu.make_async_copy(held_ref, out_hbm, sem)
    copy.start()
    copy.wait()


def finish(cells, got_ref, out_ref):
    total = jnp.sum(got_ref[...], axis=0, keepdims=True)
    out_ref[...] = jnp.sqrt(total / cells + 1e-06)


def local(right_side, reaction, velocity):
    gx, gy, gz = lax.axis_size("gx"), lax.axis_size("gy"), lax.axis_size("gz")
    shape = right_side.shape
    block = in_vmem(shape)
    face_shapes = [in_vmem(face) for face in FACES]

    def pairs(n, first):
        step = [1 - 2 * (i % 2) if first else 2 * (i % 2) - 1 for i in range(n)]
        return [(i, (i + step[i]) % n) for i in range(n)]

    def exchange_x(xa, xb):
        far = lax.ppermute(xb, "gx", pairs(gx, False))
        return [lax.ppermute(xa, "gx", pairs(gx, True)), far]

    def exchange_sides(ya, yb, zface):
        far = lax.ppermute(yb, "gy", pairs(gy, False))
        across = lax.ppermute(zface, "gz", pairs(gz, True))
        return [lax.ppermute(ya, "gy", pairs(gy, True)), far, across]

    rows = pltpu.VMEM((16, 8, 512), jnp.float32)
    faces = call(
        first_faces,
        face_shapes,
        [right_side],
        "h",
        "vvvvv",
        scratch=[rows, rows, pltpu.VMEM((16, 64, LANES), jnp.float32), pltpu.SemaphoreType.DMA((5,))],
        flops=100 * COST,
    )
    halos = exchange_x(*faces[:2]) + exchange_sides(*faces[2:])
    r, d, diag, *coefs = call(
        first_main,
        [block, block, block]
        + [in_vmem(s) for s in [(64, 512), (64, 512), (16, 8, 512), (16, 8, 512), (8, LANES)]],
        [right_side, reaction, velocity],
        "vvv",
        "v" * 8,
        flops=COST,
    )
    s = right_side
    for iteration in range(ITERS):
        if iteration > 0:
            if iteration + 1 < ITERS:
                r, d, s = call(
                    functools.partial(main, *step_factors(iteration), 1.0 / centre if iteration == 1 else None),
                    [block] * 3,
                    [d, r, s, diag, velocity],
                    "vvvvv",
                    "vvv",
                    flops=COST,
                )
            else:
                r, s = call(last_main, [block, block], [d, r, s, diag, velocity], "vvvvv", "vv", flops=COST)
        if iteration + 1 < ITERS:
            gain = step_factors(iteration)[1]
            scale = 1.0 / centre if iteration == 0 else None
            r, d, *x_faces = call(
                functools.partial(fix_ends, gain, scale),
                [block, block] + face_shapes[:2],
                [*halos, *coefs, r, d],
                "v" * 12,
                "v" * 4,
                aliases={10: 0, 11: 1},
            )
            next_halos = exchange_x(*x_faces)
            r, d, *side_faces = call(
                functools.partial(fix_inner, gain, scale),
                [block, block] + face_shapes[2:],
                [*halos[2:], *coefs[2:], r, d],
                "v" * 8,
                "v" * 5,
                aliases={6: 0, 7: 1},
            )
            halos = next_halos + exchange_sides(*side_faces)
    devices = gx * gy * gz
    residual, part = call(
        last_fix, [block, in_vmem((devices, LANES))], [*halos, *coefs, r], "v" * 11, "vv", aliases={10: 0}
    )
    solution_out = call(
        save, [pltpu.HBM(shape, jnp.float32)], [s], "v", "h", scratch=[pltpu.SemaphoreType.DMA], flops=COST
    )[0]
    part = part.reshape(devices, 1, LANES)
    got = lax.all_to_all(part, ("gx", "gy", "gz"), 0, 0, tiled=True).reshape(devices, LANES)
    cells = shape[0] * shape[1] * shape[2] * devices
    norm = call(functools.partial(finish, cells), [in_vmem((1, LANES))], [got], "v", "v")[0]
    return solution_out, residual, norm[0, 0]


def solution(mesh):
    return jax.shard_map(
        local,
        mesh=mesh,
        in_specs=(P("gx", "gy", "gz"), P("gx", "gy", "gz"), P(None, "gx", "gy", "gz")),
        out_specs=(P("gx", "gy", "gz"), P("gx", "gy", "gz"), P()),
        check_vma=False,
    )
```

profile of v0, /device:TPU:1, one launch (start us, length us, event | category | flops | bytes accessed | tf_op | source)
XLA Modules:
  0.0 70.5 jit_solution(3690743751577116131)
XLA Ops:
  0.7 1.6 %shard_map.58 = (f32[64,512]{1,0:T(8,128)S(1)}, f32[64,512]{1,0:T(8,128)S(1)}, f32[16,512]{1,0:T(8,128)S(1)}, f32[16,512]{1,0:T(8,128)S(1)}, f32[8,128]{1,0:T(8,128)S(1)}) custom-call(f32[16,64,512]{2,1,0:T(8,128)} %s_ref.1), custom_call_target="tpu_custom_call" | custom-call | flops 10000000000 | tf_op jit(solution)/shard_map/pallas_call | solution.py:46
  2.3 2.2 %collective-permute-start.3 = (f32[64,512]{1,0:T(8,128)S(1)}, f32[64,512]{1,0:T(8,128)S(1)}, u32[]{:S(2)}, u32[]{:S(2)}) collective-permute-start(f32[64,512]{1,0:T(8,128)S(1)} %get-tuple-element.71), channel_id=1, source_target_pairs={{0,8},{8,0},{16,24},{24,16},{32,40},{40,32},{48,56},{56,48},{64,72... | collective-permute-start | bytes 393224 | tf_op jit(solution)/shard_map/ppermute | solution.py:330
  4.5 4.1 %collective-permute-start.4 = (f32[64,512]{1,0:T(8,128)S(1)}, f32[64,512]{1,0:T(8,128)S(1)}, u32[]{:S(2)}, u32[]{:S(2)}) collective-permute-start(f32[64,512]{1,0:T(8,128)S(1)} %get-tuple-element.72), channel_id=1, source_target_pairs={{0,120},{8,16},{16,8},{24,32},{32,24},{40,48},{48,40},{56,64},{64,... | collective-permute-start | bytes 393224 | tf_op jit(solution)/shard_map/ppermute | solution.py:329
  8.6 1.2 %collective-permute-start = (f32[16,512]{1,0:T(8,128)S(1)}, f32[16,512]{1,0:T(8,128)S(1)}, u32[]{:S(2)}, u32[]{:S(2)}) collective-permute-start(f32[16,512]{1,0:T(8,128)S(1)} %get-tuple-element.65), channel_id=1, source_target_pairs={{0,2},{2,0},{4,6},{6,4},{1,3},{3,1},{5,7},{7,5},{8,10},{10,8},{12,... | collective-permute-start | bytes 98312 | tf_op jit(solution)/shard_map/ppermute | solution.py:335
  9.8 3.5 %collective-permute-start.1 = (f32[16,512]{1,0:T(8,128)S(1)}, f32[16,512]{1,0:T(8,128)S(1)}, u32[]{:S(2)}, u32[]{:S(2)}) collective-permute-start(f32[16,512]{1,0:T(8,128)S(1)} %get-tuple-element.66), channel_id=1, source_target_pairs={{0,6},{2,4},{4,2},{6,0},{1,7},{3,5},{5,3},{7,1},{8,14},{10,12},{12... | collective-permute-start | bytes 98312 | tf_op jit(solution)/shard_map/ppermute | solution.py:333
  13.3 0.7 %collective-permute-start.2 = (f32[8,128]{1,0:T(8,128)S(1)}, f32[8,128]{1,0:T(8,128)S(1)}, u32[]{:S(2)}, u32[]{:S(2)}) collective-permute-start(f32[8,128]{1,0:T(8,128)S(1)} %get-tuple-element.67), channel_id=1, source_target_pairs={{0,1},{1,0},{2,3},{3,2},{4,5},{5,4},{6,7},{7,6},{8,9},{9,8},{10,11... | collective-permute-start | bytes 12296 | tf_op jit(solution)/shard_map/ppermute | solution.py:334
  14.0 2.2 %shard_map.59 = (f32[16,64,512]{2,1,0:T(8,128)S(1)}, f32[16,64,512]{2,1,0:T(8,128)S(1)}, f32[16,64,512]{2,1,0:T(8,128)S(1)}, f32[64,512]{1,0:T(8,128)S(1)}, f32[...) custom-call(f32[16,64,512]{2,1,0:T(8,128)S(1)} %copy-done.1, ...), custom_call_target="tpu_custom_call" | custom-call | flops 100000000 | tf_op jit(solution)/shard_map/pallas_call | solution.py:46
  16.2 0.0 collective-permute-done.2.refs_4_.refs_2_
  16.2 0.0 collective-permute-done.refs_2_.refs_0_
  16.2 0.0 collective-permute-done.3.refs_0_
  16.2 0.0 collective-permute-done.4.refs_1_
  16.3 0.2 shard_map.60
  16.4 0.1 collective-permute-start.8
  16.5 0.8 %collective-permute-start.9 = (f32[64,512]{1,0:T(8,128)S(1)}, f32[64,512]{1,0:T(8,128)S(1)}, u32[]{:S(2)}, u32[]{:S(2)}) collective-permute-start(f32[64,512]{1,0:T(8,128)S(1)} %get-tuple-element.83), channel_id=1, source_target_pairs={{0,120},{8,16},{16,8},{24,32},{32,24},{40,48},{48,40},{56,64},{64,... | collective-permute-start | bytes 393224 | tf_op jit(solution)/shard_map/ppermute | solution.py:329
  17.3 0.5 shard_map.61
  17.9 1.8 %collective-permute-start.5 = (f32[16,512]{1,0:T(8,128)S(1)}, f32[16,512]{1,0:T(8,128)S(1)}, u32[]{:S(2)}, u32[]{:S(2)}) collective-permute-start(f32[16,512]{1,0:T(8,128)S(1)} %get-tuple-element.79), channel_id=1, source_target_pairs={{0,2},{2,0},{4,6},{6,4},{1,3},{3,1},{5,7},{7,5},{8,10},{10,8},{12,... | collective-permute-start | bytes 98312 | tf_op jit(solution)/shard_map/ppermute | solution.py:335
  19.6 3.0 %collective-permute-start.6 = (f32[16,512]{1,0:T(8,128)S(1)}, f32[16,512]{1,0:T(8,128)S(1)}, u32[]{:S(2)}, u32[]{:S(2)}) collective-permute-start(f32[16,512]{1,0:T(8,128)S(1)} %get-tuple-element.80), channel_id=1, source_target_pairs={{0,6},{2,4},{4,2},{6,0},{1,7},{3,5},{5,3},{7,1},{8,14},{10,12},{12... | collective-permute-start | bytes 98312 | tf_op jit(solution)/shard_map/ppermute | solution.py:333
  22.7 0.7 %collective-permute-start.7 = (f32[8,128]{1,0:T(8,128)S(1)}, f32[8,128]{1,0:T(8,128)S(1)}, u32[]{:S(2)}, u32[]{:S(2)}) collective-permute-start(f32[8,128]{1,0:T(8,128)S(1)} %get-tuple-element.81), channel_id=1, source_target_pairs={{0,1},{1,0},{2,3},{3,2},{4,5},{5,4},{6,7},{7,6},{8,9},{9,8},{10,11... | collective-permute-start | bytes 12296 | tf_op jit(solution)/shard_map/ppermute | solution.py:334
  23.4 2.0 %shard_map.62 = (f32[16,64,512]{2,1,0:T(8,128)S(1)}, f32[16,64,512]{2,1,0:T(8,128)S(1)}, f32[16,64,512]{2,1,0:T(8,128)S(1)}) custom-call(f32[16,64,512]{2,1,0:T(8,128)S(1)} %get-tuple-element.84.d_ref, f32[16,64,512]{2,1,0:T(8,128)S(1)} %get-tuple-element.85.r_ref, f32[16,64,512]{2,1,0:T(8,128)S(1)} %copy-done.1, ...), custom_call_target="tpu_custom_call" | custom-call | flops 100000000 | tf_op jit(solution)/shard_map/pallas_call | solution.py:46
  25.4 0.1 collective-permute-done.7.refs_4_.refs_2_
  25.5 0.0 collective-permute-done.9.refs_1_
  25.5 0.2 shard_map.63
  25.7 0.1 collective-permute-start.13
  25.7 2.9 %collective-permute-start.14 = (f32[64,512]{1,0:T(8,128)S(1)}, f32[64,512]{1,0:T(8,128)S(1)}, u32[]{:S(2)}, u32[]{:S(2)}) collective-permute-start(f32[64,512]{1,0:T(8,128)S(1)} %get-tuple-element.95), channel_id=1, source_target_pairs={{0,120},{8,16},{16,8},{24,32},{32,24},{40,48},{48,40},{56,64},{64,... | collective-permute-start | bytes 393224 | tf_op jit(solution)/shard_map/ppermute | solution.py:329
  28.7 0.6 shard_map.64
  29.3 0.5 collective-permute-start.10
  29.7 2.1 %collective-permute-start.11 = (f32[16,512]{1,0:T(8,128)S(1)}, f32[16,512]{1,0:T(8,128)S(1)}, u32[]{:S(2)}, u32[]{:S(2)}) collective-permute-start(f32[16,512]{1,0:T(8,128)S(1)} %get-tuple-element.92), channel_id=1, source_target_pairs={{0,6},{2,4},{4,2},{6,0},{1,7},{3,5},{5,3},{7,1},{8,14},{10,12},{12... | collective-permute-start | bytes 98312 | tf_op jit(solution)/shard_map/ppermute | solution.py:333
  31.8 0.7 collective-permute-start.12
  32.5 1.8 %shard_map.65 = (f32[16,64,512]{2,1,0:T(8,128)S(1)}, f32[16,64,512]{2,1,0:T(8,128)S(1)}, f32[16,64,512]{2,1,0:T(8,128)S(1)}) custom-call(f32[16,64,512]{2,1,0:T(8,128)S(1)} %get-tuple-element.96.d_ref, f32[16,64,512]{2,1,0:T(8,128)S(1)} %get-tuple-element.97.r_ref, f32[16,64,512]{2,1,0:T(8,128)S(1)} %get-tuple-element.98.s_ref, ...), custom_call_target="tpu_custom_call" | custom-call | flops 100000000 | tf_op jit(solution)/shard_map/pallas_call | solution.py:46
  34.3 0.3 collective-permute-done.12.refs_4_.refs_2_
  34.6 0.3 collective-permute-done.11.refs_3_.refs_1_
  34.9 0.0 collective-permute-done.13.refs_0_
  34.9 0.0 collective-permute-done.14.refs_1_
  34.9 0.2 shard_map.66
  35.0 0.1 collective-permute-start.18
  35.1 2.8 %collective-permute-start.19 = (f32[64,512]{1,0:T(8,128)S(1)}, f32[64,512]{1,0:T(8,128)S(1)}, u32[]{:S(2)}, u32[]{:S(2)}) collective-permute-start(f32[64,512]{1,0:T(8,128)S(1)} %get-tuple-element.107), channel_id=1, source_target_pairs={{0,120},{8,16},{16,8},{24,32},{32,24},{40,48},{48,40},{56,64},{64,... | collective-permute-start | bytes 393224 | tf_op jit(solution)/shard_map/ppermute | solution.py:329
  38.0 0.5 shard_map.67
  38.5 0.7 %collective-permute-start.15 = (f32[16,512]{1,0:T(8,128)S(1)}, f32[16,512]{1,0:T(8,128)S(1)}, u32[]{:S(2)}, u32[]{:S(2)}) collective-permute-start(f32[16,512]{1,0:T(8,128)S(1)} %get-tuple-element.103), channel_id=1, source_target_pairs={{0,2},{2,0},{4,6},{6,4},{1,3},{3,1},{5,7},{7,5},{8,10},{10,8},{12,... | collective-permute-start | bytes 98312 | tf_op jit(solution)/shard_map/ppermute | solution.py:335
  39.2 1.8 %collective-permute-start.16 = (f32[16,512]{1,0:T(8,128)S(1)}, f32[16,512]{1,0:T(8,128)S(1)}, u32[]{:S(2)}, u32[]{:S(2)}) collective-permute-start(f32[16,512]{1,0:T(8,128)S(1)} %get-tuple-element.104), channel_id=1, source_target_pairs={{0,6},{2,4},{4,2},{6,0},{1,7},{3,5},{5,3},{7,1},{8,14},{10,12},{12... | collective-permute-start | bytes 98312 | tf_op jit(solution)/shard_map/ppermute | solution.py:333
  41.0 0.7 %collective-permute-start.17 = (f32[8,128]{1,0:T(8,128)S(1)}, f32[8,128]{1,0:T(8,128)S(1)}, u32[]{:S(2)}, u32[]{:S(2)}) collective-permute-start(f32[8,128]{1,0:T(8,128)S(1)} %get-tuple-element.105), channel_id=1, source_target_pairs={{0,1},{1,0},{2,3},{3,2},{4,5},{5,4},{6,7},{7,6},{8,9},{9,8},{10,11... | collective-permute-start | bytes 12296 | tf_op jit(solution)/shard_map/ppermute | solution.py:334
  41.7 2.0 %shard_map.68 = (f32[16,64,512]{2,1,0:T(8,128)S(1)}, f32[16,64,512]{2,1,0:T(8,128)S(1)}, f32[16,64,512]{2,1,0:T(8,128)S(1)}) custom-call(f32[16,64,512]{2,1,0:T(8,128)S(1)} %get-tuple-element.108.d_ref, f32[16,64,512]{2,1,0:T(8,128)S(1)} %get-tuple-element.109.r_ref, f32[16,64,512]{2,1,0:T(8,128)S(1)} %get-tuple-element.110.s_ref, ...), custom_call_target="tpu_custom_call" | custom-call | flops 100000000 | tf_op jit(solution)/shard_map/pallas_call | solution.py:46
  43.7 0.1 collective-permute-done.17.refs_4_.refs_2_
  43.8 0.3 collective-permute-done.16.refs_3_.refs_1_
  44.1 0.0 collective-permute-done.18.refs_0_
  44.1 0.0 collective-permute-done.19.refs_1_
  44.1 0.2 shard_map.69
  44.3 0.1 collective-permute-start.20
  44.4 2.8 %collective-permute-start.21 = (f32[64,512]{1,0:T(8,128)S(1)}, f32[64,512]{1,0:T(8,128)S(1)}, u32[]{:S(2)}, u32[]{:S(2)}) collective-permute-start(f32[64,512]{1,0:T(8,128)S(1)} %get-tuple-element.120), channel_id=1, source_target_pairs={{0,120},{8,16},{16,8},{24,32},{32,24},{40,48},{48,40},{56,64},{64,... | collective-permute-start | bytes 393224 | tf_op jit(solution)/shard_map/ppermute | solution.py:329
  47.2 0.6 shard_map.70
  47.7 0.8 %collective-permute-start.22 = (f32[16,512]{1,0:T(8,128)S(1)}, f32[16,512]{1,0:T(8,128)S(1)}, u32[]{:S(2)}, u32[]{:S(2)}) collective-permute-start(f32[16,512]{1,0:T(8,128)S(1)} %get-tuple-element.121), channel_id=1, source_target_pairs={{0,2},{2,0},{4,6},{6,4},{1,3},{3,1},{5,7},{7,5},{8,10},{10,8},{12,... | collective-permute-start | bytes 98312 | tf_op jit(solution)/shard_map/ppermute | solution.py:335
  48.5 1.7 %collective-permute-start.23 = (f32[16,512]{1,0:T(8,128)S(1)}, f32[16,512]{1,0:T(8,128)S(1)}, u32[]{:S(2)}, u32[]{:S(2)}) collective-permute-start(f32[16,512]{1,0:T(8,128)S(1)} %get-tuple-element.122), channel_id=1, source_target_pairs={{0,6},{2,4},{4,2},{6,0},{1,7},{3,5},{5,3},{7,1},{8,14},{10,12},{12... | collective-permute-start | bytes 98312 | tf_op jit(solution)/shard_map/ppermute | solution.py:333
  50.2 0.7 collective-permute-start.24
  50.8 1.6 %shard_map.71 = (f32[16,64,512]{2,1,0:T(8,128)S(1)}, f32[16,64,512]{2,1,0:T(8,128)S(1)}) custom-call(f32[16,64,512]{2,1,0:T(8,128)S(1)} %get-tuple-element.115.d_ref, f32[16,64,512]{2,1,0:T(8,128)S(1)} %get-tuple-element.116.r_ref, f32[16,64,512]{2,1,0:T(8,128)S(1)} %get-tuple-element.117.s_ref, f32[16,64,512]{2,1,0:T(8,128)S(1)} %get-tuple-element.86.diag_ref, ...), custom_call_target="tpu_custom_call" | custom-call | flops 100000000 | tf_op jit(solution)/shard_map/pallas_call | solution.py:46
  52.5 0.0 copy-start.3
  52.5 0.5 collective-permute-done.24.refs_4_
  53.0 0.4 collective-permute-done.23.refs_3_
  53.3 1.3 %shard_map.73 = (f32[16,64,512]{2,1,0:T(8,128)S(1)}, f32[128,128]{1,0:T(8,128)}) custom-call(f32[64,512]{1,0:T(8,128)S(1)} %collective-permute-done.20.refs_0_, f32[64,512]{1,0:T(8,128)S(1)} %collective-permute-done.21.refs_1_, f32[16,512]{1,0:T(8,128)S(1)} %collective-permute-done.22.refs_2_, ...), custom_call_target="tpu_custom_call", output_to_operand_aliasing={{0}: (10, {})} | custom-call | tf_op jit(solution)/shard_map/pallas_call | solution.py:46
  54.7 5.8 %all-to-all-start = ((f32[128,1,128]{2,1,0:T(1,128)}), f32[128,1,128]{2,1,0:T(1,128)S(1)}, u32[]{:S(2)}, u32[]{:S(2)}) async-start(f32[128,1,128]{2,1,0:T(1,128)} %bitcast.1), calls=%async_computation | async-start | bytes 131072 | tf_op jit(solution)/shard_map/all_to_all | solution.py:400
  60.5 0.0 copy-start.4
  60.5 1.6 %copy-done.4 = f32[16,64,512]{2,1,0:T(8,128)S(1)} copy-done((f32[16,64,512]{2,1,0:T(8,128)S(1)}, f32[16,64,512]{2,1,0:T(8,128)}, u32[]{:S(2)}) %copy-start.4) | copy-done | bytes 2097176
  62.1 1.3 %shard_map.72 = f32[16,64,512]{2,1,0:T(8,128)} custom-call(f32[16,64,512]{2,1,0:T(8,128)S(1)} %copy-done.4), custom_call_target="tpu_custom_call" | custom-call | flops 100000000 | tf_op jit(solution)/shard_map/pallas_call | solution.py:46
  63.4 1.3 %copy.41 = f32[16,64,512]{2,1,0:T(8,128)} copy(f32[16,64,512]{2,1,0:T(8,128)S(1)} %get-tuple-element.128) | data formatting | bytes 4194304
  64.7 5.2 %all-to-all-done = f32[128,1,128]{2,1,0:T(1,128)S(1)} async-done(((f32[128,1,128]{2,1,0:T(1,128)}), f32[128,1,128]{2,1,0:T(1,128)S(1)}, u32[]{:S(2)}, u32[]{:S(2)}) %all-to-all-start) | async-done | bytes 65568 | tf_op jit(solution)/shard_map/all_to_all | solution.py:400
  70.0 0.5 copy-done.5
  (18 shorter events, 0.1 us)
Async XLA Ops:
  0.6 13.4 %copy-start.1 = (f32[16,64,512]{2,1,0:T(8,128)S(1)}, f32[16,64,512]{2,1,0:T(8,128)}, u32[]{:S(2)}) copy-start(f32[16,64,512]{2,1,0:T(8,128)} %s_ref.1) | copy-start | bytes 6291460
  0.6 13.4 %copy-start = (f32[3,16,64,512]{3,2,1,0:T(8,128)S(1)}, f32[3,16,64,512]{3,2,1,0:T(8,128)}, u32[]{:S(2)}) copy-start(f32[3,16,64,512]{3,2,1,0:T(8,128)} %velocity_ref.9) | copy-start | bytes 18874372
  0.7 13.4 %copy-start.2 = (f32[16,64,512]{2,1,0:T(8,128)S(1)}, f32[16,64,512]{2,1,0:T(8,128)}, u32[]{:S(2)}) copy-start(f32[16,64,512]{2,1,0:T(8,128)} %reaction_ref.1) | copy-start | bytes 6291460
  2.3 14.0 %collective-permute-start.3 = (f32[64,512]{1,0:T(8,128)S(1)}, f32[64,512]{1,0:T(8,128)S(1)}, u32[]{:S(2)}, u32[]{:S(2)}) collective-permute-start(f32[64,512]{1,0:T(8,128)S(1)} %get-tuple-element.71), channel_id=1, source_target_pairs={{0,8},{8,0},{16,24},{24,16},{32,40},{40,32},{48,56},{56,48},{64,72... | collective-permute-start | bytes 393224 | tf_op jit(solution)/shard_map/ppermute | solution.py:330
  4.5 11.8 %collective-permute-start.4 = (f32[64,512]{1,0:T(8,128)S(1)}, f32[64,512]{1,0:T(8,128)S(1)}, u32[]{:S(2)}, u32[]{:S(2)}) collective-permute-start(f32[64,512]{1,0:T(8,128)S(1)} %get-tuple-element.72), channel_id=1, source_target_pairs={{0,120},{8,16},{16,8},{24,32},{32,24},{40,48},{48,40},{56,64},{64,... | collective-permute-start | bytes 393224 | tf_op jit(solution)/shard_map/ppermute | solution.py:329
  8.6 7.6 %collective-permute-start = (f32[16,512]{1,0:T(8,128)S(1)}, f32[16,512]{1,0:T(8,128)S(1)}, u32[]{:S(2)}, u32[]{:S(2)}) collective-permute-start(f32[16,512]{1,0:T(8,128)S(1)} %get-tuple-element.65), channel_id=1, source_target_pairs={{0,2},{2,0},{4,6},{6,4},{1,3},{3,1},{5,7},{7,5},{8,10},{10,8},{12,... | collective-permute-start | bytes 98312 | tf_op jit(solution)/shard_map/ppermute | solution.py:335
  9.8 6.4 %collective-permute-start.1 = (f32[16,512]{1,0:T(8,128)S(1)}, f32[16,512]{1,0:T(8,128)S(1)}, u32[]{:S(2)}, u32[]{:S(2)}) collective-permute-start(f32[16,512]{1,0:T(8,128)S(1)} %get-tuple-element.66), channel_id=1, source_target_pairs={{0,6},{2,4},{4,2},{6,0},{1,7},{3,5},{5,3},{7,1},{8,14},{10,12},{12... | collective-permute-start | bytes 98312 | tf_op jit(solution)/shard_map/ppermute | solution.py:333
  13.3 2.9 %collective-permute-start.2 = (f32[8,128]{1,0:T(8,128)S(1)}, f32[8,128]{1,0:T(8,128)S(1)}, u32[]{:S(2)}, u32[]{:S(2)}) collective-permute-start(f32[8,128]{1,0:T(8,128)S(1)} %get-tuple-element.67), channel_id=1, source_target_pairs={{0,1},{1,0},{2,3},{3,2},{4,5},{5,4},{6,7},{7,6},{8,9},{9,8},{10,11... | collective-permute-start | bytes 12296 | tf_op jit(solution)/shard_map/ppermute | solution.py:334
  16.4 9.0 %collective-permute-start.8 = (f32[64,512]{1,0:T(8,128)S(1)}, f32[64,512]{1,0:T(8,128)S(1)}, u32[]{:S(2)}, u32[]{:S(2)}) collective-permute-start(f32[64,512]{1,0:T(8,128)S(1)} %get-tuple-element.82), channel_id=1, source_target_pairs={{0,8},{8,0},{16,24},{24,16},{32,40},{40,32},{48,56},{56,48},{64,72... | collective-permute-start | bytes 393224 | tf_op jit(solution)/shard_map/ppermute | solution.py:330
  16.5 8.9 %collective-permute-start.9 = (f32[64,512]{1,0:T(8,128)S(1)}, f32[64,512]{1,0:T(8,128)S(1)}, u32[]{:S(2)}, u32[]{:S(2)}) collective-permute-start(f32[64,512]{1,0:T(8,128)S(1)} %get-tuple-element.83), channel_id=1, source_target_pairs={{0,120},{8,16},{16,8},{24,32},{32,24},{40,48},{48,40},{56,64},{64,... | collective-permute-start | bytes 393224 | tf_op jit(solution)/shard_map/ppermute | solution.py:329
  17.9 7.6 %collective-permute-start.5 = (f32[16,512]{1,0:T(8,128)S(1)}, f32[16,512]{1,0:T(8,128)S(1)}, u32[]{:S(2)}, u32[]{:S(2)}) collective-permute-start(f32[16,512]{1,0:T(8,128)S(1)} %get-tuple-element.79), channel_id=1, source_target_pairs={{0,2},{2,0},{4,6},{6,4},{1,3},{3,1},{5,7},{7,5},{8,10},{10,8},{12,... | collective-permute-start | bytes 98312 | tf_op jit(solution)/shard_map/ppermute | solution.py:335
  19.6 5.8 %collective-permute-start.6 = (f32[16,512]{1,0:T(8,128)S(1)}, f32[16,512]{1,0:T(8,128)S(1)}, u32[]{:S(2)}, u32[]{:S(2)}) collective-permute-start(f32[16,512]{1,0:T(8,128)S(1)} %get-tuple-element.80), channel_id=1, source_target_pairs={{0,6},{2,4},{4,2},{6,0},{1,7},{3,5},{5,3},{7,1},{8,14},{10,12},{12... | collective-permute-start | bytes 98312 | tf_op jit(solution)/shard_map/ppermute | solution.py:333
  22.7 2.8 %collective-permute-start.7 = (f32[8,128]{1,0:T(8,128)S(1)}, f32[8,128]{1,0:T(8,128)S(1)}, u32[]{:S(2)}, u32[]{:S(2)}) collective-permute-start(f32[8,128]{1,0:T(8,128)S(1)} %get-tuple-element.81), channel_id=1, source_target_pairs={{0,1},{1,0},{2,3},{3,2},{4,5},{5,4},{6,7},{7,6},{8,9},{9,8},{10,11... | collective-permute-start | bytes 12296 | tf_op jit(solution)/shard_map/ppermute | solution.py:334
  25.7 9.2 %collective-permute-start.13 = (f32[64,512]{1,0:T(8,128)S(1)}, f32[64,512]{1,0:T(8,128)S(1)}, u32[]{:S(2)}, u32[]{:S(2)}) collective-permute-start(f32[64,512]{1,0:T(8,128)S(1)} %get-tuple-element.94), channel_id=1, source_target_pairs={{0,8},{8,0},{16,24},{24,16},{32,40},{40,32},{48,56},{56,48},{64,72... | collective-permute-start | bytes 393224 | tf_op jit(solution)/shard_map/ppermute | solution.py:330
  25.7 9.1 %collective-permute-start.14 = (f32[64,512]{1,0:T(8,128)S(1)}, f32[64,512]{1,0:T(8,128)S(1)}, u32[]{:S(2)}, u32[]{:S(2)}) collective-permute-start(f32[64,512]{1,0:T(8,128)S(1)} %get-tuple-element.95), channel_id=1, source_target_pairs={{0,120},{8,16},{16,8},{24,32},{32,24},{40,48},{48,40},{56,64},{64,... | collective-permute-start | bytes 393224 | tf_op jit(solution)/shard_map/ppermute | solution.py:329
  29.3 5.3 %collective-permute-start.10 = (f32[16,512]{1,0:T(8,128)S(1)}, f32[16,512]{1,0:T(8,128)S(1)}, u32[]{:S(2)}, u32[]{:S(2)}) collective-permute-start(f32[16,512]{1,0:T(8,128)S(1)} %get-tuple-element.91), channel_id=1, source_target_pairs={{0,2},{2,0},{4,6},{6,4},{1,3},{3,1},{5,7},{7,5},{8,10},{10,8},{12,... | collective-permute-start | bytes 98312 | tf_op jit(solution)/shard_map/ppermute | solution.py:335
  29.7 5.1 %collective-permute-start.11 = (f32[16,512]{1,0:T(8,128)S(1)}, f32[16,512]{1,0:T(8,128)S(1)}, u32[]{:S(2)}, u32[]{:S(2)}) collective-permute-start(f32[16,512]{1,0:T(8,128)S(1)} %get-tuple-element.92), channel_id=1, source_target_pairs={{0,6},{2,4},{4,2},{6,0},{1,7},{3,5},{5,3},{7,1},{8,14},{10,12},{12... | collective-permute-start | bytes 98312 | tf_op jit(solution)/shard_map/ppermute | solution.py:333
  31.8 2.8 %collective-permute-start.12 = (f32[8,128]{1,0:T(8,128)S(1)}, f32[8,128]{1,0:T(8,128)S(1)}, u32[]{:S(2)}, u32[]{:S(2)}) collective-permute-start(f32[8,128]{1,0:T(8,128)S(1)} %get-tuple-element.93), channel_id=1, source_target_pairs={{0,1},{1,0},{2,3},{3,2},{4,5},{5,4},{6,7},{7,6},{8,9},{9,8},{10,11... | collective-permute-start | bytes 12296 | tf_op jit(solution)/shard_map/ppermute | solution.py:334
  35.0 9.1 %collective-permute-start.18 = (f32[64,512]{1,0:T(8,128)S(1)}, f32[64,512]{1,0:T(8,128)S(1)}, u32[]{:S(2)}, u32[]{:S(2)}) collective-permute-start(f32[64,512]{1,0:T(8,128)S(1)} %get-tuple-element.106), channel_id=1, source_target_pairs={{0,8},{8,0},{16,24},{24,16},{32,40},{40,32},{48,56},{56,48},{64,72... | collective-permute-start | bytes 393224 | tf_op jit(solution)/shard_map/ppermute | solution.py:330
  35.1 9.0 %collective-permute-start.19 = (f32[64,512]{1,0:T(8,128)S(1)}, f32[64,512]{1,0:T(8,128)S(1)}, u32[]{:S(2)}, u32[]{:S(2)}) collective-permute-start(f32[64,512]{1,0:T(8,128)S(1)} %get-tuple-element.107), channel_id=1, source_target_pairs={{0,120},{8,16},{16,8},{24,32},{32,24},{40,48},{48,40},{56,64},{64,... | collective-permute-start | bytes 393224 | tf_op jit(solution)/shard_map/ppermute | solution.py:329
  38.5 5.3 %collective-permute-start.15 = (f32[16,512]{1,0:T(8,128)S(1)}, f32[16,512]{1,0:T(8,128)S(1)}, u32[]{:S(2)}, u32[]{:S(2)}) collective-permute-start(f32[16,512]{1,0:T(8,128)S(1)} %get-tuple-element.103), channel_id=1, source_target_pairs={{0,2},{2,0},{4,6},{6,4},{1,3},{3,1},{5,7},{7,5},{8,10},{10,8},{12,... | collective-permute-start | bytes 98312 | tf_op jit(solution)/shard_map/ppermute | solution.py:335
  39.2 4.9 %collective-permute-start.16 = (f32[16,512]{1,0:T(8,128)S(1)}, f32[16,512]{1,0:T(8,128)S(1)}, u32[]{:S(2)}, u32[]{:S(2)}) collective-permute-start(f32[16,512]{1,0:T(8,128)S(1)} %get-tuple-element.104), channel_id=1, source_target_pairs={{0,6},{2,4},{4,2},{6,0},{1,7},{3,5},{5,3},{7,1},{8,14},{10,12},{12... | collective-permute-start | bytes 98312 | tf_op jit(solution)/shard_map/ppermute | solution.py:333
  41.0 2.8 %collective-permute-start.17 = (f32[8,128]{1,0:T(8,128)S(1)}, f32[8,128]{1,0:T(8,128)S(1)}, u32[]{:S(2)}, u32[]{:S(2)}) collective-permute-start(f32[8,128]{1,0:T(8,128)S(1)} %get-tuple-element.105), channel_id=1, source_target_pairs={{0,1},{1,0},{2,3},{3,2},{4,5},{5,4},{6,7},{7,6},{8,9},{9,8},{10,11... | collective-permute-start | bytes 12296 | tf_op jit(solution)/shard_map/ppermute | solution.py:334
  44.3 9.1 %collective-permute-start.20 = (f32[64,512]{1,0:T(8,128)S(1)}, f32[64,512]{1,0:T(8,128)S(1)}, u32[]{:S(2)}, u32[]{:S(2)}) collective-permute-start(f32[64,512]{1,0:T(8,128)S(1)} %get-tuple-element.119), channel_id=1, source_target_pairs={{0,8},{8,0},{16,24},{24,16},{32,40},{40,32},{48,56},{56,48},{64,72... | collective-permute-start | bytes 393224 | tf_op jit(solution)/shard_map/ppermute | solution.py:330
  44.4 9.0 %collective-permute-start.21 = (f32[64,512]{1,0:T(8,128)S(1)}, f32[64,512]{1,0:T(8,128)S(1)}, u32[]{:S(2)}, u32[]{:S(2)}) collective-permute-start(f32[64,512]{1,0:T(8,128)S(1)} %get-tuple-element.120), channel_id=1, source_target_pairs={{0,120},{8,16},{16,8},{24,32},{32,24},{40,48},{48,40},{56,64},{64,... | collective-permute-start | bytes 393224 | tf_op jit(solution)/shard_map/ppermute | solution.py:329
  47.7 5.2 %collective-permute-start.22 = (f32[16,512]{1,0:T(8,128)S(1)}, f32[16,512]{1,0:T(8,128)S(1)}, u32[]{:S(2)}, u32[]{:S(2)}) collective-permute-start(f32[16,512]{1,0:T(8,128)S(1)} %get-tuple-element.121), channel_id=1, source_target_pairs={{0,2},{2,0},{4,6},{6,4},{1,3},{3,1},{5,7},{7,5},{8,10},{10,8},{12,... | collective-permute-start | bytes 98312 | tf_op jit(solution)/shard_map/ppermute | solution.py:335
  48.5 4.8 %collective-permute-start.23 = (f32[16,512]{1,0:T(8,128)S(1)}, f32[16,512]{1,0:T(8,128)S(1)}, u32[]{:S(2)}, u32[]{:S(2)}) collective-permute-start(f32[16,512]{1,0:T(8,128)S(1)} %get-tuple-element.122), channel_id=1, source_target_pairs={{0,6},{2,4},{4,2},{6,0},{1,7},{3,5},{5,3},{7,1},{8,14},{10,12},{12... | collective-permute-start | bytes 98312 | tf_op jit(solution)/shard_map/ppermute | solution.py:333
  50.2 2.8 %collective-permute-start.24 = (f32[8,128]{1,0:T(8,128)S(1)}, f32[8,128]{1,0:T(8,128)S(1)}, u32[]{:S(2)}, u32[]{:S(2)}) collective-permute-start(f32[8,128]{1,0:T(8,128)S(1)} %get-tuple-element.123), channel_id=1, source_target_pairs={{0,1},{1,0},{2,3},{3,2},{4,5},{5,4},{6,7},{7,6},{8,9},{9,8},{10,11... | collective-permute-start | bytes 12296 | tf_op jit(solution)/shard_map/ppermute | solution.py:334
  52.5 2.2 %copy-start.3 = (f32[16,64,512]{2,1,0:T(8,128)}, f32[16,64,512]{2,1,0:T(8,128)S(1)}, u32[]{:S(2)}) copy-start(f32[16,64,512]{2,1,0:T(8,128)S(1)} %get-tuple-element.118.held_ref) | copy-start | bytes 6291460
  54.7 15.3 %all-to-all-start = ((f32[128,1,128]{2,1,0:T(1,128)}), f32[128,1,128]{2,1,0:T(1,128)S(1)}, u32[]{:S(2)}, u32[]{:S(2)}) async-start(f32[128,1,128]{2,1,0:T(1,128)} %bitcast.1), calls=%async_computation | async-start | bytes 131072 | tf_op jit(solution)/shard_map/all_to_all | solution.py:400
  60.5 1.6 %copy-start.4 = (f32[16,64,512]{2,1,0:T(8,128)S(1)}, f32[16,64,512]{2,1,0:T(8,128)}, u32[]{:S(2)}) copy-start(f32[16,64,512]{2,1,0:T(8,128)} %copy-done.3) | copy-start | bytes 6291460
  69.9 0.5 copy-start.5
where the time goes:
time: 70.6 us; the launch traced here: 70.5 us
  starting transfers between devices  42.3 us (60%)
  Pallas kernels  16.8 us (24%)
  waiting for transfers between devices  7.11 us (10%)
  local copies, waits for them, and re-layouts  3.44 us (5%)
  between operations  0.84 us (1%)
    pallas_call x17, Pallas kernels, call(): pl.pallas_call(body, out_shape=out_shape, in_specs=[spec[space] for space...  16.8 us
    ppermute x5, starting transfers between devices, exchange_x(): far = lax.ppermute(xb, 'gx', pairs(gx, False))  13.4 us
    ppermute x5, starting transfers between devices, exchange_sides(): far = lax.ppermute(yb, 'gy', pairs(gy, False))  12 us
    all_to_all x1, starting transfers between devices, local(): lax.all_to_all(part, ('gx', 'gy', 'gz'), 0, 0, tiled=True)  5.8 us
    all_to_all x1, waiting for transfers between devices, local(): lax.all_to_all(part, ('gx', 'gy', 'gz'), 0, 0, tiled=True)  5.21 us
    ppermute x5, starting transfers between devices, exchange_sides(): return [lax.ppermute(ya, 'gy', pairs(gy, True)), far, across]  4.95 us
    ppermute x5, starting transfers between devices, exchange_sides(): across = lax.ppermute(zface, 'gz', pairs(gz, True))  3.53 us
    unnamed x13, local copies, waits for them, and re-layouts  3.44 us
  transfers between devices with their start and end apart: 26, of which 8 were waited for; matrix products, arithmetic and copies ran while one was open for 2% of the time, Pallas kernels for 19%

commit v1 on v0

--- a/solution.py
+++ b/solution.py
@@ -106,29 +106,27 @@
 FACES = [(64, 512), (64, 512), (16, 512), (16, 512), (8, LANES)]
 
 
-def first_faces(rhs_hbm, xa, xb, ya, yb, zface, rows_a, rows_b, column, sem):
-    place = position()
-    planes, rows, tiles = sides(place)
-    offset, _ = column_tile(place)
+def first_x_faces(rhs_hbm, xa, xb, sem):
+    planes, _, _ = sides(position())
     copies = [
-        pltpu.make_async_copy(rhs_hbm.at[:, :, pl.ds(offset, LANES)], column, sem.at[0]),
-        pltpu.make_async_copy(rhs_hbm.at[:, pl.ds(tiles[0], 8), :], rows_a, sem.at[1]),
-        pltpu.make_async_copy(rhs_hbm.at[:, pl.ds(tiles[1], 8), :], rows_b, sem.at[2]),
-        pltpu.make_async_copy(rhs_hbm.at[planes[0]], xa, sem.at[3]),
-        pltpu.make_async_copy(rhs_hbm.at[planes[1]], xb, sem.at[4]),
+        pltpu.make_async_copy(rhs_hbm.at[planes[0]], xa, sem.at[0]),
+        pltpu.make_async_copy(rhs_hbm.at[planes[1]], xb, sem.at[1]),
     ]
     for copy in copies:
         copy.start()
-    for copy in copies[:3]:
+    for copy in copies:
         copy.wait()
-    held = rows_a, rows_b
+
+
+def first_side_faces(rhs_ref, ya, yb, zface):
+    place = position()
+    _, rows, _ = sides(place)
+    offset, _ = column_tile(place)
     write_side_faces(
-        lambda n, i: held[n][i, pl.ds(lax.rem(rows[n], 8), 1), :],
-        lambda i, t: column[i, 8 * t : 8 * t + 8, :],
+        lambda n, i: rhs_ref[i, pl.ds(rows[n], 1), :],
+        lambda i, t: rhs_ref[i, 8 * t : 8 * t + 8, pl.ds(offset, LANES)],
         place, ya, yb, zface,
     )
-    for copy in copies[3:]:
-        copy.wait()
 
 
 def row_of_tiles(ref, i, t):
@@ -334,17 +332,18 @@
         across = lax.ppermute(zface, "gz", pairs(gz, True))
         return [lax.ppermute(ya, "gy", pairs(gy, True)), far, across]
 
-    rows = pltpu.VMEM((16, 8, 512), jnp.float32)
-    faces = call(
-        first_faces,
-        face_shapes,
+    x_faces = call(
+        first_x_faces,
+        face_shapes[:2],
         [right_side],
         "h",
-        "vvvvv",
-        scratch=[rows, rows, pltpu.VMEM((16, 64, LANES), jnp.float32), pltpu.SemaphoreType.DMA((5,))],
+        "vv",
+        scratch=[pltpu.SemaphoreType.DMA((2,))],
         flops=100 * COST,
     )
-    halos = exchange_x(*faces[:2]) + exchange_sides(*faces[2:])
+    halos = exchange_x(*x_faces)
+    side_faces = call(first_side_faces, face_shapes[2:], [right_side], "v", "vvv")
+    halos += exchange_sides(*side_faces)
     r, d, diag, *coefs = call(
         first_main,
         [block, block, block]

time: 70.6 us -> 70.2 us (level)
    pallas_call x17 -> x18, Pallas kernels: 16.8 us -> 16.6 us  [call(): pl.pallas_call(body, out_shape=out_shape, in_specs=[spec[space] for space...]
where the time goes in v1:
time: 70.2 us; the launch traced here: 70 us
  starting transfers between devices  42 us (60%)
  Pallas kernels  16.6 us (24%)
  waiting for transfers between devices  7.1 us (10%)
  local copies, waits for them, and re-layouts  3.44 us (5%)
  between operations  0.85 us (1%)
    pallas_call x18, Pallas kernels, call(): pl.pallas_call(body, out_shape=out_shape, in_specs=[spec[space] for space...  16.6 us
    ppermute x5, starting transfers between devices, exchange_x(): far = lax.ppermute(xb, 'gx', pairs(gx, False))  13.8 us
    ppermute x5, starting transfers between devices, exchange_sides(): far = lax.ppermute(yb, 'gy', pairs(gy, False))  11.6 us
    all_to_all x1, starting transfers between devices, local(): lax.all_to_all(part, ('gx', 'gy', 'gz'), 0, 0, tiled=True)  5.59 us
    all_to_all x1, waiting for transfers between devices, local(): lax.all_to_all(part, ('gx', 'gy', 'gz'), 0, 0, tiled=True)  5.19 us
    ppermute x5, starting transfers between devices, exchange_sides(): return [lax.ppermute(ya, 'gy', pairs(gy, True)), far, across]  4.94 us
    ppermute x5, starting transfers between devices, exchange_sides(): across = lax.ppermute(zface, 'gz', pairs(gz, True))  3.61 us
    unnamed x13, local copies, waits for them, and re-layouts  3.44 us
  transfers between devices with their start and end apart: 26, of which 8 were waited for; matrix products, arithmetic and copies ran while one was open for 2% of the time, Pallas kernels for 19%

profile of v1, /device:TPU:1, one launch (start us, length us, event | category | flops | bytes accessed | tf_op | source)
XLA Modules:
  0.0 70.0 jit_solution(13583018994107273728)
XLA Ops:
  0.6 1.1 %shard_map.60 = (f32[64,512]{1,0:T(8,128)S(1)}, f32[64,512]{1,0:T(8,128)S(1)}) custom-call(f32[16,64,512]{2,1,0:T(8,128)} %s_ref.1), custom_call_target="tpu_custom_call" | custom-call | flops 10000000000 | tf_op jit(solution)/shard_map/pallas_call | solution.py:46
  1.8 0.0 copy-start.2
  1.8 2.2 %collective-permute-start.3 = (f32[64,512]{1,0:T(8,128)S(1)}, f32[64,512]{1,0:T(8,128)S(1)}, u32[]{:S(2)}, u32[]{:S(2)}) collective-permute-start(f32[64,512]{1,0:T(8,128)S(1)} %get-tuple-element.71), channel_id=1, source_target_pairs={{0,8},{8,0},{16,24},{24,16},{32,40},{40,32},{48,56},{56,48},{64,72... | collective-permute-start | bytes 393224 | tf_op jit(solution)/shard_map/ppermute | solution.py:328
  4.0 4.1 %collective-permute-start.4 = (f32[64,512]{1,0:T(8,128)S(1)}, f32[64,512]{1,0:T(8,128)S(1)}, u32[]{:S(2)}, u32[]{:S(2)}) collective-permute-start(f32[64,512]{1,0:T(8,128)S(1)} %get-tuple-element.72), channel_id=1, source_target_pairs={{0,120},{8,16},{16,8},{24,32},{32,24},{40,48},{48,40},{56,64},{64,... | collective-permute-start | bytes 393224 | tf_op jit(solution)/shard_map/ppermute | solution.py:327
  8.1 0.2 shard_map.58
  8.3 1.3 %collective-permute-start = (f32[16,512]{1,0:T(8,128)S(1)}, f32[16,512]{1,0:T(8,128)S(1)}, u32[]{:S(2)}, u32[]{:S(2)}) collective-permute-start(f32[16,512]{1,0:T(8,128)S(1)} %get-tuple-element.65), channel_id=1, source_target_pairs={{0,2},{2,0},{4,6},{6,4},{1,3},{3,1},{5,7},{7,5},{8,10},{10,8},{12,... | collective-permute-start | bytes 98312 | tf_op jit(solution)/shard_map/ppermute | solution.py:333
  9.7 3.6 %collective-permute-start.1 = (f32[16,512]{1,0:T(8,128)S(1)}, f32[16,512]{1,0:T(8,128)S(1)}, u32[]{:S(2)}, u32[]{:S(2)}) collective-permute-start(f32[16,512]{1,0:T(8,128)S(1)} %get-tuple-element.66), channel_id=1, source_target_pairs={{0,6},{2,4},{4,2},{6,0},{1,7},{3,5},{5,3},{7,1},{8,14},{10,12},{12... | collective-permute-start | bytes 98312 | tf_op jit(solution)/shard_map/ppermute | solution.py:331
  13.2 0.7 %collective-permute-start.2 = (f32[8,128]{1,0:T(8,128)S(1)}, f32[8,128]{1,0:T(8,128)S(1)}, u32[]{:S(2)}, u32[]{:S(2)}) collective-permute-start(f32[8,128]{1,0:T(8,128)S(1)} %get-tuple-element.67), channel_id=1, source_target_pairs={{0,1},{1,0},{2,3},{3,2},{4,5},{5,4},{6,7},{7,6},{8,9},{9,8},{10,11... | collective-permute-start | bytes 12296 | tf_op jit(solution)/shard_map/ppermute | solution.py:332
  14.0 2.2 %shard_map.59 = (f32[16,64,512]{2,1,0:T(8,128)S(1)}, f32[16,64,512]{2,1,0:T(8,128)S(1)}, f32[16,64,512]{2,1,0:T(8,128)S(1)}, f32[64,512]{1,0:T(8,128)S(1)}, f32[...) custom-call(f32[16,64,512]{2,1,0:T(8,128)S(1)} %copy-done.1, ...), custom_call_target="tpu_custom_call" | custom-call | flops 100000000 | tf_op jit(solution)/shard_map/pallas_call | solution.py:46
  16.2 0.0 collective-permute-done.1.refs_3_.refs_1_
  16.2 0.2 shard_map.61
  16.4 0.1 collective-permute-start.8
  16.5 0.8 %collective-permute-start.9 = (f32[64,512]{1,0:T(8,128)S(1)}, f32[64,512]{1,0:T(8,128)S(1)}, u32[]{:S(2)}, u32[]{:S(2)}) collective-permute-start(f32[64,512]{1,0:T(8,128)S(1)} %get-tuple-element.83), channel_id=1, source_target_pairs={{0,120},{8,16},{16,8},{24,32},{32,24},{40,48},{48,40},{56,64},{64,... | collective-permute-start | bytes 393224 | tf_op jit(solution)/shard_map/ppermute | solution.py:327
  17.3 0.6 shard_map.62
  17.9 1.6 %collective-permute-start.5 = (f32[16,512]{1,0:T(8,128)S(1)}, f32[16,512]{1,0:T(8,128)S(1)}, u32[]{:S(2)}, u32[]{:S(2)}) collective-permute-start(f32[16,512]{1,0:T(8,128)S(1)} %get-tuple-element.79), channel_id=1, source_target_pairs={{0,2},{2,0},{4,6},{6,4},{1,3},{3,1},{5,7},{7,5},{8,10},{10,8},{12,... | collective-permute-start | bytes 98312 | tf_op jit(solution)/shard_map/ppermute | solution.py:333
  19.5 2.7 %collective-permute-start.6 = (f32[16,512]{1,0:T(8,128)S(1)}, f32[16,512]{1,0:T(8,128)S(1)}, u32[]{:S(2)}, u32[]{:S(2)}) collective-permute-start(f32[16,512]{1,0:T(8,128)S(1)} %get-tuple-element.80), channel_id=1, source_target_pairs={{0,6},{2,4},{4,2},{6,0},{1,7},{3,5},{5,3},{7,1},{8,14},{10,12},{12... | collective-permute-start | bytes 98312 | tf_op jit(solution)/shard_map/ppermute | solution.py:331
  22.2 0.7 %collective-permute-start.7 = (f32[8,128]{1,0:T(8,128)S(1)}, f32[8,128]{1,0:T(8,128)S(1)}, u32[]{:S(2)}, u32[]{:S(2)}) collective-permute-start(f32[8,128]{1,0:T(8,128)S(1)} %get-tuple-element.81), channel_id=1, source_target_pairs={{0,1},{1,0},{2,3},{3,2},{4,5},{5,4},{6,7},{7,6},{8,9},{9,8},{10,11... | collective-permute-start | bytes 12296 | tf_op jit(solution)/shard_map/ppermute | solution.py:332
  23.0 2.0 %shard_map.63 = (f32[16,64,512]{2,1,0:T(8,128)S(1)}, f32[16,64,512]{2,1,0:T(8,128)S(1)}, f32[16,64,512]{2,1,0:T(8,128)S(1)}) custom-call(f32[16,64,512]{2,1,0:T(8,128)S(1)} %get-tuple-element.84.d_ref, f32[16,64,512]{2,1,0:T(8,128)S(1)} %get-tuple-element.85.r_ref, f32[16,64,512]{2,1,0:T(8,128)S(1)} %copy-done.1, ...), custom_call_target="tpu_custom_call" | custom-call | flops 100000000 | tf_op jit(solution)/shard_map/pallas_call | solution.py:46
  24.9 0.1 collective-permute-done.7.refs_4_.refs_2_
  25.0 0.0 collective-permute-done.5.refs_2_.refs_0_
  25.0 0.0 collective-permute-done.6.refs_3_.refs_1_
  25.0 0.0 collective-permute-done.8.refs_0_
  25.1 0.0 collective-permute-done.9.refs_1_
  25.1 0.2 shard_map.64
  25.2 0.1 collective-permute-start.13
  25.3 3.2 %collective-permute-start.14 = (f32[64,512]{1,0:T(8,128)S(1)}, f32[64,512]{1,0:T(8,128)S(1)}, u32[]{:S(2)}, u32[]{:S(2)}) collective-permute-start(f32[64,512]{1,0:T(8,128)S(1)} %get-tuple-element.95), channel_id=1, source_target_pairs={{0,120},{8,16},{16,8},{24,32},{32,24},{40,48},{48,40},{56,64},{64,... | collective-permute-start | bytes 393224 | tf_op jit(solution)/shard_map/ppermute | solution.py:327
  28.6 0.6 shard_map.65
  29.1 0.5 collective-permute-start.10
  29.6 2.0 %collective-permute-start.11 = (f32[16,512]{1,0:T(8,128)S(1)}, f32[16,512]{1,0:T(8,128)S(1)}, u32[]{:S(2)}, u32[]{:S(2)}) collective-permute-start(f32[16,512]{1,0:T(8,128)S(1)} %get-tuple-element.92), channel_id=1, source_target_pairs={{0,6},{2,4},{4,2},{6,0},{1,7},{3,5},{5,3},{7,1},{8,14},{10,12},{12... | collective-permute-start | bytes 98312 | tf_op jit(solution)/shard_map/ppermute | solution.py:331
  31.6 0.7 %collective-permute-start.12 = (f32[8,128]{1,0:T(8,128)S(1)}, f32[8,128]{1,0:T(8,128)S(1)}, u32[]{:S(2)}, u32[]{:S(2)}) collective-permute-start(f32[8,128]{1,0:T(8,128)S(1)} %get-tuple-element.93), channel_id=1, source_target_pairs={{0,1},{1,0},{2,3},{3,2},{4,5},{5,4},{6,7},{7,6},{8,9},{9,8},{10,11... | collective-permute-start | bytes 12296 | tf_op jit(solution)/shard_map/ppermute | solution.py:332
  32.4 1.8 %shard_map.66 = (f32[16,64,512]{2,1,0:T(8,128)S(1)}, f32[16,64,512]{2,1,0:T(8,128)S(1)}, f32[16,64,512]{2,1,0:T(8,128)S(1)}) custom-call(f32[16,64,512]{2,1,0:T(8,128)S(1)} %get-tuple-element.96.d_ref, f32[16,64,512]{2,1,0:T(8,128)S(1)} %get-tuple-element.97.r_ref, f32[16,64,512]{2,1,0:T(8,128)S(1)} %get-tuple-element.98.s_ref, ...), custom_call_target="tpu_custom_call" | custom-call | flops 100000000 | tf_op jit(solution)/shard_map/pallas_call | solution.py:46
  34.2 0.2 collective-permute-done.12.refs_4_.refs_2_
  34.4 0.0 collective-permute-done.10.refs_2_.refs_0_
  34.4 0.1 collective-permute-done.11.refs_3_.refs_1_
  34.5 0.0 collective-permute-done.13.refs_0_
  34.5 0.2 shard_map.67
  34.7 0.1 collective-permute-start.18
  34.8 3.0 %collective-permute-start.19 = (f32[64,512]{1,0:T(8,128)S(1)}, f32[64,512]{1,0:T(8,128)S(1)}, u32[]{:S(2)}, u32[]{:S(2)}) collective-permute-start(f32[64,512]{1,0:T(8,128)S(1)} %get-tuple-element.107), channel_id=1, source_target_pairs={{0,120},{8,16},{16,8},{24,32},{32,24},{40,48},{48,40},{56,64},{64,... | collective-permute-start | bytes 393224 | tf_op jit(solution)/shard_map/ppermute | solution.py:327
  37.8 0.5 shard_map.68
  38.3 0.8 %collective-permute-start.15 = (f32[16,512]{1,0:T(8,128)S(1)}, f32[16,512]{1,0:T(8,128)S(1)}, u32[]{:S(2)}, u32[]{:S(2)}) collective-permute-start(f32[16,512]{1,0:T(8,128)S(1)} %get-tuple-element.103), channel_id=1, source_target_pairs={{0,2},{2,0},{4,6},{6,4},{1,3},{3,1},{5,7},{7,5},{8,10},{10,8},{12,... | collective-permute-start | bytes 98312 | tf_op jit(solution)/shard_map/ppermute | solution.py:333
  39.1 1.5 %collective-permute-start.16 = (f32[16,512]{1,0:T(8,128)S(1)}, f32[16,512]{1,0:T(8,128)S(1)}, u32[]{:S(2)}, u32[]{:S(2)}) collective-permute-start(f32[16,512]{1,0:T(8,128)S(1)} %get-tuple-element.104), channel_id=1, source_target_pairs={{0,6},{2,4},{4,2},{6,0},{1,7},{3,5},{5,3},{7,1},{8,14},{10,12},{12... | collective-permute-start | bytes 98312 | tf_op jit(solution)/shard_map/ppermute | solution.py:331
  40.6 0.7 %collective-permute-start.17 = (f32[8,128]{1,0:T(8,128)S(1)}, f32[8,128]{1,0:T(8,128)S(1)}, u32[]{:S(2)}, u32[]{:S(2)}) collective-permute-start(f32[8,128]{1,0:T(8,128)S(1)} %get-tuple-element.105), channel_id=1, source_target_pairs={{0,1},{1,0},{2,3},{3,2},{4,5},{5,4},{6,7},{7,6},{8,9},{9,8},{10,11... | collective-permute-start | bytes 12296 | tf_op jit(solution)/shard_map/ppermute | solution.py:332
  41.3 2.0 %shard_map.69 = (f32[16,64,512]{2,1,0:T(8,128)S(1)}, f32[16,64,512]{2,1,0:T(8,128)S(1)}, f32[16,64,512]{2,1,0:T(8,128)S(1)}) custom-call(f32[16,64,512]{2,1,0:T(8,128)S(1)} %get-tuple-element.108.d_ref, f32[16,64,512]{2,1,0:T(8,128)S(1)} %get-tuple-element.109.r_ref, f32[16,64,512]{2,1,0:T(8,128)S(1)} %get-tuple-element.110.s_ref, ...), custom_call_target="tpu_custom_call" | custom-call | flops 100000000 | tf_op jit(solution)/shard_map/pallas_call | solution.py:46
  43.3 0.1 collective-permute-done.17.refs_4_.refs_2_
  43.4 0.5 collective-permute-done.16.refs_3_.refs_1_
  43.9 0.2 shard_map.70
  44.1 0.1 collective-permute-start.20
  44.2 2.7 %collective-permute-start.21 = (f32[64,512]{1,0:T(8,128)S(1)}, f32[64,512]{1,0:T(8,128)S(1)}, u32[]{:S(2)}, u32[]{:S(2)}) collective-permute-start(f32[64,512]{1,0:T(8,128)S(1)} %get-tuple-element.120), channel_id=1, source_target_pairs={{0,120},{8,16},{16,8},{24,32},{32,24},{40,48},{48,40},{56,64},{64,... | collective-permute-start | bytes 393224 | tf_op jit(solution)/shard_map/ppermute | solution.py:327
  46.9 0.6 shard_map.71
  47.5 0.8 %collective-permute-start.22 = (f32[16,512]{1,0:T(8,128)S(1)}, f32[16,512]{1,0:T(8,128)S(1)}, u32[]{:S(2)}, u32[]{:S(2)}) collective-permute-start(f32[16,512]{1,0:T(8,128)S(1)} %get-tuple-element.121), channel_id=1, source_target_pairs={{0,2},{2,0},{4,6},{6,4},{1,3},{3,1},{5,7},{7,5},{8,10},{10,8},{12,... | collective-permute-start | bytes 98312 | tf_op jit(solution)/shard_map/ppermute | solution.py:333
  48.3 1.7 %collective-permute-start.23 = (f32[16,512]{1,0:T(8,128)S(1)}, f32[16,512]{1,0:T(8,128)S(1)}, u32[]{:S(2)}, u32[]{:S(2)}) collective-permute-start(f32[16,512]{1,0:T(8,128)S(1)} %get-tuple-element.122), channel_id=1, source_target_pairs={{0,6},{2,4},{4,2},{6,0},{1,7},{3,5},{5,3},{7,1},{8,14},{10,12},{12... | collective-permute-start | bytes 98312 | tf_op jit(solution)/shard_map/ppermute | solution.py:331
  50.0 0.7 %collective-permute-start.24 = (f32[8,128]{1,0:T(8,128)S(1)}, f32[8,128]{1,0:T(8,128)S(1)}, u32[]{:S(2)}, u32[]{:S(2)}) collective-permute-start(f32[8,128]{1,0:T(8,128)S(1)} %get-tuple-element.123), channel_id=1, source_target_pairs={{0,1},{1,0},{2,3},{3,2},{4,5},{5,4},{6,7},{7,6},{8,9},{9,8},{10,11... | collective-permute-start | bytes 12296 | tf_op jit(solution)/shard_map/ppermute | solution.py:332
  50.7 1.6 %shard_map.72 = (f32[16,64,512]{2,1,0:T(8,128)S(1)}, f32[16,64,512]{2,1,0:T(8,128)S(1)}) custom-call(f32[16,64,512]{2,1,0:T(8,128)S(1)} %get-tuple-element.115.d_ref, f32[16,64,512]{2,1,0:T(8,128)S(1)} %get-tuple-element.116.r_ref, f32[16,64,512]{2,1,0:T(8,128)S(1)} %get-tuple-element.117.s_ref, f32[16,64,512]{2,1,0:T(8,128)S(1)} %get-tuple-element.86.diag_ref, ...), custom_call_target="tpu_custom_call" | custom-call | flops 100000000 | tf_op jit(solution)/shard_map/pallas_call | solution.py:46
  52.4 0.0 copy-start.3
  52.4 0.4 collective-permute-done.24.refs_4_
  52.8 0.3 collective-permute-done.23.refs_3_
  53.1 1.3 %shard_map.74 = (f32[16,64,512]{2,1,0:T(8,128)S(1)}, f32[128,128]{1,0:T(8,128)}) custom-call(f32[64,512]{1,0:T(8,128)S(1)} %collective-permute-done.20.refs_0_, f32[64,512]{1,0:T(8,128)S(1)} %collective-permute-done.21.refs_1_, f32[16,512]{1,0:T(8,128)S(1)} %collective-permute-done.22.refs_2_, ...), custom_call_target="tpu_custom_call", output_to_operand_aliasing={{0}: (10, {})} | custom-call | tf_op jit(solution)/shard_map/pallas_call | solution.py:46
  54.5 5.6 %all-to-all-start = ((f32[128,1,128]{2,1,0:T(1,128)}), f32[128,1,128]{2,1,0:T(1,128)S(1)}, u32[]{:S(2)}, u32[]{:S(2)}) async-start(f32[128,1,128]{2,1,0:T(1,128)} %bitcast.1), calls=%async_computation | async-start | bytes 131072 | tf_op jit(solution)/shard_map/all_to_all | solution.py:399
  60.0 0.0 copy-start.4
  60.1 1.6 %copy-done.4 = f32[16,64,512]{2,1,0:T(8,128)S(1)} copy-done((f32[16,64,512]{2,1,0:T(8,128)S(1)}, f32[16,64,512]{2,1,0:T(8,128)}, u32[]{:S(2)}) %copy-start.4) | copy-done | bytes 2097176
  61.6 1.3 %shard_map.73 = f32[16,64,512]{2,1,0:T(8,128)} custom-call(f32[16,64,512]{2,1,0:T(8,128)S(1)} %copy-done.4), custom_call_target="tpu_custom_call" | custom-call | flops 100000000 | tf_op jit(solution)/shard_map/pallas_call | solution.py:46
  63.0 1.3 %copy.41 = f32[16,64,512]{2,1,0:T(8,128)} copy(f32[16,64,512]{2,1,0:T(8,128)S(1)} %get-tuple-element.128) | data formatting | bytes 4194304
  64.3 5.2 %all-to-all-done = f32[128,1,128]{2,1,0:T(1,128)S(1)} async-done(((f32[128,1,128]{2,1,0:T(1,128)}), f32[128,1,128]{2,1,0:T(1,128)S(1)}, u32[]{:S(2)}, u32[]{:S(2)}) %all-to-all-start) | async-done | bytes 65568 | tf_op jit(solution)/shard_map/all_to_all | solution.py:399
  69.5 0.5 copy-done.5
  (19 shorter events, 0.1 us)
Async XLA Ops:
  0.6 7.5 %copy-start.1 = (f32[16,64,512]{2,1,0:T(8,128)S(1)}, f32[16,64,512]{2,1,0:T(8,128)}, u32[]{:S(2)}) copy-start(f32[16,64,512]{2,1,0:T(8,128)} %s_ref.1) | copy-start | bytes 6291460
  0.6 13.3 %copy-start = (f32[3,16,64,512]{3,2,1,0:T(8,128)S(1)}, f32[3,16,64,512]{3,2,1,0:T(8,128)}, u32[]{:S(2)}) copy-start(f32[3,16,64,512]{3,2,1,0:T(8,128)} %velocity_ref.9) | copy-start | bytes 18874372
  1.8 12.2 %copy-start.2 = (f32[16,64,512]{2,1,0:T(8,128)S(1)}, f32[16,64,512]{2,1,0:T(8,128)}, u32[]{:S(2)}) copy-start(f32[16,64,512]{2,1,0:T(8,128)} %reaction_ref.1) | copy-start | bytes 6291460
  1.8 14.4 %collective-permute-start.3 = (f32[64,512]{1,0:T(8,128)S(1)}, f32[64,512]{1,0:T(8,128)S(1)}, u32[]{:S(2)}, u32[]{:S(2)}) collective-permute-start(f32[64,512]{1,0:T(8,128)S(1)} %get-tuple-element.71), channel_id=1, source_target_pairs={{0,8},{8,0},{16,24},{24,16},{32,40},{40,32},{48,56},{56,48},{64,72... | collective-permute-start | bytes 393224 | tf_op jit(solution)/shard_map/ppermute | solution.py:328
  4.0 12.2 %collective-permute-start.4 = (f32[64,512]{1,0:T(8,128)S(1)}, f32[64,512]{1,0:T(8,128)S(1)}, u32[]{:S(2)}, u32[]{:S(2)}) collective-permute-start(f32[64,512]{1,0:T(8,128)S(1)} %get-tuple-element.72), channel_id=1, source_target_pairs={{0,120},{8,16},{16,8},{24,32},{32,24},{40,48},{48,40},{56,64},{64,... | collective-permute-start | bytes 393224 | tf_op jit(solution)/shard_map/ppermute | solution.py:327
  8.3 7.9 %collective-permute-start = (f32[16,512]{1,0:T(8,128)S(1)}, f32[16,512]{1,0:T(8,128)S(1)}, u32[]{:S(2)}, u32[]{:S(2)}) collective-permute-start(f32[16,512]{1,0:T(8,128)S(1)} %get-tuple-element.65), channel_id=1, source_target_pairs={{0,2},{2,0},{4,6},{6,4},{1,3},{3,1},{5,7},{7,5},{8,10},{10,8},{12,... | collective-permute-start | bytes 98312 | tf_op jit(solution)/shard_map/ppermute | solution.py:333
  9.7 6.6 %collective-permute-start.1 = (f32[16,512]{1,0:T(8,128)S(1)}, f32[16,512]{1,0:T(8,128)S(1)}, u32[]{:S(2)}, u32[]{:S(2)}) collective-permute-start(f32[16,512]{1,0:T(8,128)S(1)} %get-tuple-element.66), channel_id=1, source_target_pairs={{0,6},{2,4},{4,2},{6,0},{1,7},{3,5},{5,3},{7,1},{8,14},{10,12},{12... | collective-permute-start | bytes 98312 | tf_op jit(solution)/shard_map/ppermute | solution.py:331
  13.2 3.0 %collective-permute-start.2 = (f32[8,128]{1,0:T(8,128)S(1)}, f32[8,128]{1,0:T(8,128)S(1)}, u32[]{:S(2)}, u32[]{:S(2)}) collective-permute-start(f32[8,128]{1,0:T(8,128)S(1)} %get-tuple-element.67), channel_id=1, source_target_pairs={{0,1},{1,0},{2,3},{3,2},{4,5},{5,4},{6,7},{7,6},{8,9},{9,8},{10,11... | collective-permute-start | bytes 12296 | tf_op jit(solution)/shard_map/ppermute | solution.py:332
  16.4 8.6 %collective-permute-start.8 = (f32[64,512]{1,0:T(8,128)S(1)}, f32[64,512]{1,0:T(8,128)S(1)}, u32[]{:S(2)}, u32[]{:S(2)}) collective-permute-start(f32[64,512]{1,0:T(8,128)S(1)} %get-tuple-element.82), channel_id=1, source_target_pairs={{0,8},{8,0},{16,24},{24,16},{32,40},{40,32},{48,56},{56,48},{64,72... | collective-permute-start | bytes 393224 | tf_op jit(solution)/shard_map/ppermute | solution.py:328
  16.5 8.5 %collective-permute-start.9 = (f32[64,512]{1,0:T(8,128)S(1)}, f32[64,512]{1,0:T(8,128)S(1)}, u32[]{:S(2)}, u32[]{:S(2)}) collective-permute-start(f32[64,512]{1,0:T(8,128)S(1)} %get-tuple-element.83), channel_id=1, source_target_pairs={{0,120},{8,16},{16,8},{24,32},{32,24},{40,48},{48,40},{56,64},{64,... | collective-permute-start | bytes 393224 | tf_op jit(solution)/shard_map/ppermute | solution.py:327
  17.9 7.2 %collective-permute-start.5 = (f32[16,512]{1,0:T(8,128)S(1)}, f32[16,512]{1,0:T(8,128)S(1)}, u32[]{:S(2)}, u32[]{:S(2)}) collective-permute-start(f32[16,512]{1,0:T(8,128)S(1)} %get-tuple-element.79), channel_id=1, source_target_pairs={{0,2},{2,0},{4,6},{6,4},{1,3},{3,1},{5,7},{7,5},{8,10},{10,8},{12,... | collective-permute-start | bytes 98312 | tf_op jit(solution)/shard_map/ppermute | solution.py:333
  19.5 5.5 %collective-permute-start.6 = (f32[16,512]{1,0:T(8,128)S(1)}, f32[16,512]{1,0:T(8,128)S(1)}, u32[]{:S(2)}, u32[]{:S(2)}) collective-permute-start(f32[16,512]{1,0:T(8,128)S(1)} %get-tuple-element.80), channel_id=1, source_target_pairs={{0,6},{2,4},{4,2},{6,0},{1,7},{3,5},{5,3},{7,1},{8,14},{10,12},{12... | collective-permute-start | bytes 98312 | tf_op jit(solution)/shard_map/ppermute | solution.py:331
  22.2 2.8 %collective-permute-start.7 = (f32[8,128]{1,0:T(8,128)S(1)}, f32[8,128]{1,0:T(8,128)S(1)}, u32[]{:S(2)}, u32[]{:S(2)}) collective-permute-start(f32[8,128]{1,0:T(8,128)S(1)} %get-tuple-element.81), channel_id=1, source_target_pairs={{0,1},{1,0},{2,3},{3,2},{4,5},{5,4},{6,7},{7,6},{8,9},{9,8},{10,11... | collective-permute-start | bytes 12296 | tf_op jit(solution)/shard_map/ppermute | solution.py:332
  25.2 9.3 %collective-permute-start.13 = (f32[64,512]{1,0:T(8,128)S(1)}, f32[64,512]{1,0:T(8,128)S(1)}, u32[]{:S(2)}, u32[]{:S(2)}) collective-permute-start(f32[64,512]{1,0:T(8,128)S(1)} %get-tuple-element.94), channel_id=1, source_target_pairs={{0,8},{8,0},{16,24},{24,16},{32,40},{40,32},{48,56},{56,48},{64,72... | collective-permute-start | bytes 393224 | tf_op jit(solution)/shard_map/ppermute | solution.py:328
  25.3 9.2 %collective-permute-start.14 = (f32[64,512]{1,0:T(8,128)S(1)}, f32[64,512]{1,0:T(8,128)S(1)}, u32[]{:S(2)}, u32[]{:S(2)}) collective-permute-start(f32[64,512]{1,0:T(8,128)S(1)} %get-tuple-element.95), channel_id=1, source_target_pairs={{0,120},{8,16},{16,8},{24,32},{32,24},{40,48},{48,40},{56,64},{64,... | collective-permute-start | bytes 393224 | tf_op jit(solution)/shard_map/ppermute | solution.py:327
  29.1 5.3 %collective-permute-start.10 = (f32[16,512]{1,0:T(8,128)S(1)}, f32[16,512]{1,0:T(8,128)S(1)}, u32[]{:S(2)}, u32[]{:S(2)}) collective-permute-start(f32[16,512]{1,0:T(8,128)S(1)} %get-tuple-element.91), channel_id=1, source_target_pairs={{0,2},{2,0},{4,6},{6,4},{1,3},{3,1},{5,7},{7,5},{8,10},{10,8},{12,... | collective-permute-start | bytes 98312 | tf_op jit(solution)/shard_map/ppermute | solution.py:333
  29.6 4.9 %collective-permute-start.11 = (f32[16,512]{1,0:T(8,128)S(1)}, f32[16,512]{1,0:T(8,128)S(1)}, u32[]{:S(2)}, u32[]{:S(2)}) collective-permute-start(f32[16,512]{1,0:T(8,128)S(1)} %get-tuple-element.92), channel_id=1, source_target_pairs={{0,6},{2,4},{4,2},{6,0},{1,7},{3,5},{5,3},{7,1},{8,14},{10,12},{12... | collective-permute-start | bytes 98312 | tf_op jit(solution)/shard_map/ppermute | solution.py:331
  31.6 2.8 %collective-permute-start.12 = (f32[8,128]{1,0:T(8,128)S(1)}, f32[8,128]{1,0:T(8,128)S(1)}, u32[]{:S(2)}, u32[]{:S(2)}) collective-permute-start(f32[8,128]{1,0:T(8,128)S(1)} %get-tuple-element.93), channel_id=1, source_target_pairs={{0,1},{1,0},{2,3},{3,2},{4,5},{5,4},{6,7},{7,6},{8,9},{9,8},{10,11... | collective-permute-start | bytes 12296 | tf_op jit(solution)/shard_map/ppermute | solution.py:332
  34.7 9.2 %collective-permute-start.18 = (f32[64,512]{1,0:T(8,128)S(1)}, f32[64,512]{1,0:T(8,128)S(1)}, u32[]{:S(2)}, u32[]{:S(2)}) collective-permute-start(f32[64,512]{1,0:T(8,128)S(1)} %get-tuple-element.106), channel_id=1, source_target_pairs={{0,8},{8,0},{16,24},{24,16},{32,40},{40,32},{48,56},{56,48},{64,72... | collective-permute-start | bytes 393224 | tf_op jit(solution)/shard_map/ppermute | solution.py:328
  34.8 9.1 %collective-permute-start.19 = (f32[64,512]{1,0:T(8,128)S(1)}, f32[64,512]{1,0:T(8,128)S(1)}, u32[]{:S(2)}, u32[]{:S(2)}) collective-permute-start(f32[64,512]{1,0:T(8,128)S(1)} %get-tuple-element.107), channel_id=1, source_target_pairs={{0,120},{8,16},{16,8},{24,32},{32,24},{40,48},{48,40},{56,64},{64,... | collective-permute-start | bytes 393224 | tf_op jit(solution)/shard_map/ppermute | solution.py:327
  38.3 5.1 %collective-permute-start.15 = (f32[16,512]{1,0:T(8,128)S(1)}, f32[16,512]{1,0:T(8,128)S(1)}, u32[]{:S(2)}, u32[]{:S(2)}) collective-permute-start(f32[16,512]{1,0:T(8,128)S(1)} %get-tuple-element.103), channel_id=1, source_target_pairs={{0,2},{2,0},{4,6},{6,4},{1,3},{3,1},{5,7},{7,5},{8,10},{10,8},{12,... | collective-permute-start | bytes 98312 | tf_op jit(solution)/shard_map/ppermute | solution.py:333
  39.1 4.9 %collective-permute-start.16 = (f32[16,512]{1,0:T(8,128)S(1)}, f32[16,512]{1,0:T(8,128)S(1)}, u32[]{:S(2)}, u32[]{:S(2)}) collective-permute-start(f32[16,512]{1,0:T(8,128)S(1)} %get-tuple-element.104), channel_id=1, source_target_pairs={{0,6},{2,4},{4,2},{6,0},{1,7},{3,5},{5,3},{7,1},{8,14},{10,12},{12... | collective-permute-start | bytes 98312 | tf_op jit(solution)/shard_map/ppermute | solution.py:331
  40.6 2.8 %collective-permute-start.17 = (f32[8,128]{1,0:T(8,128)S(1)}, f32[8,128]{1,0:T(8,128)S(1)}, u32[]{:S(2)}, u32[]{:S(2)}) collective-permute-start(f32[8,128]{1,0:T(8,128)S(1)} %get-tuple-element.105), channel_id=1, source_target_pairs={{0,1},{1,0},{2,3},{3,2},{4,5},{5,4},{6,7},{7,6},{8,9},{9,8},{10,11... | collective-permute-start | bytes 12296 | tf_op jit(solution)/shard_map/ppermute | solution.py:332
  44.1 9.0 %collective-permute-start.20 = (f32[64,512]{1,0:T(8,128)S(1)}, f32[64,512]{1,0:T(8,128)S(1)}, u32[]{:S(2)}, u32[]{:S(2)}) collective-permute-start(f32[64,512]{1,0:T(8,128)S(1)} %get-tuple-element.119), channel_id=1, source_target_pairs={{0,8},{8,0},{16,24},{24,16},{32,40},{40,32},{48,56},{56,48},{64,72... | collective-permute-start | bytes 393224 | tf_op jit(solution)/shard_map/ppermute | solution.py:328
  44.2 8.9 %collective-permute-start.21 = (f32[64,512]{1,0:T(8,128)S(1)}, f32[64,512]{1,0:T(8,128)S(1)}, u32[]{:S(2)}, u32[]{:S(2)}) collective-permute-start(f32[64,512]{1,0:T(8,128)S(1)} %get-tuple-element.120), channel_id=1, source_target_pairs={{0,120},{8,16},{16,8},{24,32},{32,24},{40,48},{48,40},{56,64},{64,... | collective-permute-start | bytes 393224 | tf_op jit(solution)/shard_map/ppermute | solution.py:327
  47.5 5.3 %collective-permute-start.22 = (f32[16,512]{1,0:T(8,128)S(1)}, f32[16,512]{1,0:T(8,128)S(1)}, u32[]{:S(2)}, u32[]{:S(2)}) collective-permute-start(f32[16,512]{1,0:T(8,128)S(1)} %get-tuple-element.121), channel_id=1, source_target_pairs={{0,2},{2,0},{4,6},{6,4},{1,3},{3,1},{5,7},{7,5},{8,10},{10,8},{12,... | collective-permute-start | bytes 98312 | tf_op jit(solution)/shard_map/ppermute | solution.py:333
  48.3 4.9 %collective-permute-start.23 = (f32[16,512]{1,0:T(8,128)S(1)}, f32[16,512]{1,0:T(8,128)S(1)}, u32[]{:S(2)}, u32[]{:S(2)}) collective-permute-start(f32[16,512]{1,0:T(8,128)S(1)} %get-tuple-element.122), channel_id=1, source_target_pairs={{0,6},{2,4},{4,2},{6,0},{1,7},{3,5},{5,3},{7,1},{8,14},{10,12},{12... | collective-permute-start | bytes 98312 | tf_op jit(solution)/shard_map/ppermute | solution.py:331
  50.0 2.8 %collective-permute-start.24 = (f32[8,128]{1,0:T(8,128)S(1)}, f32[8,128]{1,0:T(8,128)S(1)}, u32[]{:S(2)}, u32[]{:S(2)}) collective-permute-start(f32[8,128]{1,0:T(8,128)S(1)} %get-tuple-element.123), channel_id=1, source_target_pairs={{0,1},{1,0},{2,3},{3,2},{4,5},{5,4},{6,7},{7,6},{8,9},{9,8},{10,11... | collective-permute-start | bytes 12296 | tf_op jit(solution)/shard_map/ppermute | solution.py:332
  52.4 2.1 %copy-start.3 = (f32[16,64,512]{2,1,0:T(8,128)}, f32[16,64,512]{2,1,0:T(8,128)S(1)}, u32[]{:S(2)}) copy-start(f32[16,64,512]{2,1,0:T(8,128)S(1)} %get-tuple-element.118.held_ref) | copy-start | bytes 6291460
  54.5 15.0 %all-to-all-start = ((f32[128,1,128]{2,1,0:T(1,128)}), f32[128,1,128]{2,1,0:T(1,128)S(1)}, u32[]{:S(2)}, u32[]{:S(2)}) async-start(f32[128,1,128]{2,1,0:T(1,128)} %bitcast.1), calls=%async_computation | async-start | bytes 131072 | tf_op jit(solution)/shard_map/all_to_all | solution.py:399
  60.0 1.6 %copy-start.4 = (f32[16,64,512]{2,1,0:T(8,128)S(1)}, f32[16,64,512]{2,1,0:T(8,128)}, u32[]{:S(2)}) copy-start(f32[16,64,512]{2,1,0:T(8,128)} %copy-done.3) | copy-start | bytes 6291460
  69.5 0.5 copy-start.5

commit v2 on v1

--- a/solution.py
+++ b/solution.py
@@ -292,14 +292,14 @@
     _, r_ref, part_ref = refs[10:]
     correct(None, position(), None, halos, coefs, r_ref, None, True, True)
 
-    def plane(i, total):
+    totals = [jnp.zeros((8, 512), jnp.float32)] * 4
+    for i in range(16):
         for t in range(8):
             value = r_ref[i, 8 * t : 8 * t + 8, :]
-            total = total + value * value
-        return total
-
-    total = lax.fori_loop(0, 16, plane, jnp.zeros((8, 512), jnp.float32), unroll=2)
-    part_ref[...] = jnp.broadcast_to(jnp.sum(total).reshape(1, 1), part_ref.shape)
+            totals[t % 4] = totals[t % 4] + value * value
+    total = (totals[0] + totals[1]) + (totals[2] + totals[3])
+    lanes = (total[:, :128] + total[:, 128:256]) + (total[:, 256:384] + total[:, 384:])
+    part_ref[...] = jnp.broadcast_to(jnp.sum(lanes, axis=0, keepdims=True), part_ref.shape)
 
 
 def save(held_ref, out_hbm, sem):
@@ -309,8 +309,8 @@
 
 
 def finish(cells, got_ref, out_ref):
-    total = jnp.sum(got_ref[...], axis=0, keepdims=True)
-    out_ref[...] = jnp.sqrt(total / cells + 1e-06)
+    total = jnp.sum(jnp.sum(got_ref[...], axis=0, keepdims=True), axis=1, keepdims=True)
+    out_ref[...] = jnp.broadcast_to(jnp.sqrt(total / cells + 1e-06), out_ref.shape)
 
 
 def local(right_side, reaction, velocity):

time: 70.2 us -> 70.2 us (level)
  no operation moved by 1% of the time
where the time goes in v2:
time: 70.2 us; the launch traced here: 70 us
  starting transfers between devices  42 us (60%)
  Pallas kernels  16.6 us (24%)
  waiting for transfers between devices  7.1 us (10%)
  local copies, waits for them, and re-layouts  3.44 us (5%)
  between operations  0.84 us (1%)
    pallas_call x18, Pallas kernels, call(): pl.pallas_call(body, out_shape=out_shape, in_specs=[spec[space] for space...  16.6 us
    ppermute x5, starting transfers between devices, exchange_x(): far = lax.ppermute(xb, 'gx', pairs(gx, False))  13.8 us
    ppermute x5, starting transfers between devices, exchange_sides(): far = lax.ppermute(yb, 'gy', pairs(gy, False))  11.6 us
    all_to_all x1, starting transfers between devices, local(): lax.all_to_all(part, ('gx', 'gy', 'gz'), 0, 0, tiled=True)  5.58 us
    all_to_all x1, waiting for transfers between devices, local(): lax.all_to_all(part, ('gx', 'gy', 'gz'), 0, 0, tiled=True)  5.19 us
    ppermute x5, starting transfers between devices, exchange_sides(): return [lax.ppermute(ya, 'gy', pairs(gy, True)), far, across]  4.94 us
    ppermute x5, starting transfers between devices, exchange_sides(): across = lax.ppermute(zface, 'gz', pairs(gz, True))  3.61 us
    unnamed x13, local copies, waits for them, and re-layouts  3.44 us
  transfers between devices with their start and end apart: 26, of which 8 were waited for; matrix products, arithmetic and copies ran while one was open for 2% of the time, Pallas kernels for 19%

profile of v2, /device:TPU:1, one launch (start us, length us, event | category | flops | bytes accessed | tf_op | source)
XLA Modules:
  0.0 70.0 jit_solution(12730857772317312254)
XLA Ops:
  0.6 1.1 %shard_map.60 = (f32[64,512]{1,0:T(8,128)S(1)}, f32[64,512]{1,0:T(8,128)S(1)}) custom-call(f32[16,64,512]{2,1,0:T(8,128)} %s_ref.1), custom_call_target="tpu_custom_call" | custom-call | flops 10000000000 | tf_op jit(solution)/shard_map/pallas_call | solution.py:46
  1.8 0.0 copy-start.2
  1.8 2.2 %collective-permute-start.3 = (f32[64,512]{1,0:T(8,128)S(1)}, f32[64,512]{1,0:T(8,128)S(1)}, u32[]{:S(2)}, u32[]{:S(2)}) collective-permute-start(f32[64,512]{1,0:T(8,128)S(1)} %get-tuple-element.71), channel_id=1, source_target_pairs={{0,8},{8,0},{16,24},{24,16},{32,40},{40,32},{48,56},{56,48},{64,72... | collective-permute-start | bytes 393224 | tf_op jit(solution)/shard_map/ppermute | solution.py:328
  4.0 4.1 %collective-permute-start.4 = (f32[64,512]{1,0:T(8,128)S(1)}, f32[64,512]{1,0:T(8,128)S(1)}, u32[]{:S(2)}, u32[]{:S(2)}) collective-permute-start(f32[64,512]{1,0:T(8,128)S(1)} %get-tuple-element.72), channel_id=1, source_target_pairs={{0,120},{8,16},{16,8},{24,32},{32,24},{40,48},{48,40},{56,64},{64,... | collective-permute-start | bytes 393224 | tf_op jit(solution)/shard_map/ppermute | solution.py:327
  8.1 0.2 shard_map.58
  8.3 1.3 %collective-permute-start = (f32[16,512]{1,0:T(8,128)S(1)}, f32[16,512]{1,0:T(8,128)S(1)}, u32[]{:S(2)}, u32[]{:S(2)}) collective-permute-start(f32[16,512]{1,0:T(8,128)S(1)} %get-tuple-element.65), channel_id=1, source_target_pairs={{0,2},{2,0},{4,6},{6,4},{1,3},{3,1},{5,7},{7,5},{8,10},{10,8},{12,... | collective-permute-start | bytes 98312 | tf_op jit(solution)/shard_map/ppermute | solution.py:333
  9.7 3.6 %collective-permute-start.1 = (f32[16,512]{1,0:T(8,128)S(1)}, f32[16,512]{1,0:T(8,128)S(1)}, u32[]{:S(2)}, u32[]{:S(2)}) collective-permute-start(f32[16,512]{1,0:T(8,128)S(1)} %get-tuple-element.66), channel_id=1, source_target_pairs={{0,6},{2,4},{4,2},{6,0},{1,7},{3,5},{5,3},{7,1},{8,14},{10,12},{12... | collective-permute-start | bytes 98312 | tf_op jit(solution)/shard_map/ppermute | solution.py:331
  13.2 0.7 %collective-permute-start.2 = (f32[8,128]{1,0:T(8,128)S(1)}, f32[8,128]{1,0:T(8,128)S(1)}, u32[]{:S(2)}, u32[]{:S(2)}) collective-permute-start(f32[8,128]{1,0:T(8,128)S(1)} %get-tuple-element.67), channel_id=1, source_target_pairs={{0,1},{1,0},{2,3},{3,2},{4,5},{5,4},{6,7},{7,6},{8,9},{9,8},{10,11... | collective-permute-start | bytes 12296 | tf_op jit(solution)/shard_map/ppermute | solution.py:332
  14.0 2.2 %shard_map.59 = (f32[16,64,512]{2,1,0:T(8,128)S(1)}, f32[16,64,512]{2,1,0:T(8,128)S(1)}, f32[16,64,512]{2,1,0:T(8,128)S(1)}, f32[64,512]{1,0:T(8,128)S(1)}, f32[...) custom-call(f32[16,64,512]{2,1,0:T(8,128)S(1)} %copy-done.1, ...), custom_call_target="tpu_custom_call" | custom-call | flops 100000000 | tf_op jit(solution)/shard_map/pallas_call | solution.py:46
  16.2 0.0 collective-permute-done.1.refs_3_.refs_1_
  16.2 0.2 shard_map.61
  16.4 0.1 collective-permute-start.8
  16.5 0.8 %collective-permute-start.9 = (f32[64,512]{1,0:T(8,128)S(1)}, f32[64,512]{1,0:T(8,128)S(1)}, u32[]{:S(2)}, u32[]{:S(2)}) collective-permute-start(f32[64,512]{1,0:T(8,128)S(1)} %get-tuple-element.83), channel_id=1, source_target_pairs={{0,120},{8,16},{16,8},{24,32},{32,24},{40,48},{48,40},{56,64},{64,... | collective-permute-start | bytes 393224 | tf_op jit(solution)/shard_map/ppermute | solution.py:327
  17.3 0.6 shard_map.62
  17.9 1.6 %collective-permute-start.5 = (f32[16,512]{1,0:T(8,128)S(1)}, f32[16,512]{1,0:T(8,128)S(1)}, u32[]{:S(2)}, u32[]{:S(2)}) collective-permute-start(f32[16,512]{1,0:T(8,128)S(1)} %get-tuple-element.79), channel_id=1, source_target_pairs={{0,2},{2,0},{4,6},{6,4},{1,3},{3,1},{5,7},{7,5},{8,10},{10,8},{12,... | collective-permute-start | bytes 98312 | tf_op jit(solution)/shard_map/ppermute | solution.py:333
  19.5 2.7 %collective-permute-start.6 = (f32[16,512]{1,0:T(8,128)S(1)}, f32[16,512]{1,0:T(8,128)S(1)}, u32[]{:S(2)}, u32[]{:S(2)}) collective-permute-start(f32[16,512]{1,0:T(8,128)S(1)} %get-tuple-element.80), channel_id=1, source_target_pairs={{0,6},{2,4},{4,2},{6,0},{1,7},{3,5},{5,3},{7,1},{8,14},{10,12},{12... | collective-permute-start | bytes 98312 | tf_op jit(solution)/shard_map/ppermute | solution.py:331
  22.2 0.7 %collective-permute-start.7 = (f32[8,128]{1,0:T(8,128)S(1)}, f32[8,128]{1,0:T(8,128)S(1)}, u32[]{:S(2)}, u32[]{:S(2)}) collective-permute-start(f32[8,128]{1,0:T(8,128)S(1)} %get-tuple-element.81), channel_id=1, source_target_pairs={{0,1},{1,0},{2,3},{3,2},{4,5},{5,4},{6,7},{7,6},{8,9},{9,8},{10,11... | collective-permute-start | bytes 12296 | tf_op jit(solution)/shard_map/ppermute | solution.py:332
  23.0 2.0 %shard_map.63 = (f32[16,64,512]{2,1,0:T(8,128)S(1)}, f32[16,64,512]{2,1,0:T(8,128)S(1)}, f32[16,64,512]{2,1,0:T(8,128)S(1)}) custom-call(f32[16,64,512]{2,1,0:T(8,128)S(1)} %get-tuple-element.84.d_ref, f32[16,64,512]{2,1,0:T(8,128)S(1)} %get-tuple-element.85.r_ref, f32[16,64,512]{2,1,0:T(8,128)S(1)} %copy-done.1, ...), custom_call_target="tpu_custom_call" | custom-call | flops 100000000 | tf_op jit(solution)/shard_map/pallas_call | solution.py:46
  24.9 0.1 collective-permute-done.7.refs_4_.refs_2_
  25.0 0.0 collective-permute-done.5.refs_2_.refs_0_
  25.0 0.0 collective-permute-done.6.refs_3_.refs_1_
  25.0 0.0 collective-permute-done.8.refs_0_
  25.1 0.0 collective-permute-done.9.refs_1_
  25.1 0.2 shard_map.64
  25.2 0.1 collective-permute-start.13
  25.3 3.2 %collective-permute-start.14 = (f32[64,512]{1,0:T(8,128)S(1)}, f32[64,512]{1,0:T(8,128)S(1)}, u32[]{:S(2)}, u32[]{:S(2)}) collective-permute-start(f32[64,512]{1,0:T(8,128)S(1)} %get-tuple-element.95), channel_id=1, source_target_pairs={{0,120},{8,16},{16,8},{24,32},{32,24},{40,48},{48,40},{56,64},{64,... | collective-permute-start | bytes 393224 | tf_op jit(solution)/shard_map/ppermute | solution.py:327
  28.6 0.6 shard_map.65
  29.1 0.5 collective-permute-start.10
  29.6 2.0 %collective-permute-start.11 = (f32[16,512]{1,0:T(8,128)S(1)}, f32[16,512]{1,0:T(8,128)S(1)}, u32[]{:S(2)}, u32[]{:S(2)}) collective-permute-start(f32[16,512]{1,0:T(8,128)S(1)} %get-tuple-element.92), channel_id=1, source_target_pairs={{0,6},{2,4},{4,2},{6,0},{1,7},{3,5},{5,3},{7,1},{8,14},{10,12},{12... | collective-permute-start | bytes 98312 | tf_op jit(solution)/shard_map/ppermute | solution.py:331
  31.6 0.7 %collective-permute-start.12 = (f32[8,128]{1,0:T(8,128)S(1)}, f32[8,128]{1,0:T(8,128)S(1)}, u32[]{:S(2)}, u32[]{:S(2)}) collective-permute-start(f32[8,128]{1,0:T(8,128)S(1)} %get-tuple-element.93), channel_id=1, source_target_pairs={{0,1},{1,0},{2,3},{3,2},{4,5},{5,4},{6,7},{7,6},{8,9},{9,8},{10,11... | collective-permute-start | bytes 12296 | tf_op jit(solution)/shard_map/ppermute | solution.py:332
  32.4 1.8 %shard_map.66 = (f32[16,64,512]{2,1,0:T(8,128)S(1)}, f32[16,64,512]{2,1,0:T(8,128)S(1)}, f32[16,64,512]{2,1,0:T(8,128)S(1)}) custom-call(f32[16,64,512]{2,1,0:T(8,128)S(1)} %get-tuple-element.96.d_ref, f32[16,64,512]{2,1,0:T(8,128)S(1)} %get-tuple-element.97.r_ref, f32[16,64,512]{2,1,0:T(8,128)S(1)} %get-tuple-element.98.s_ref, ...), custom_call_target="tpu_custom_call" | custom-call | flops 100000000 | tf_op jit(solution)/shard_map/pallas_call | solution.py:46
  34.2 0.2 collective-permute-done.12.refs_4_.refs_2_
  34.4 0.0 collective-permute-done.10.refs_2_.refs_0_
  34.4 0.1 collective-permute-done.11.refs_3_.refs_1_
  34.5 0.2 shard_map.67
  34.7 0.1 collective-permute-start.18
  34.8 3.0 %collective-permute-start.19 = (f32[64,512]{1,0:T(8,128)S(1)}, f32[64,512]{1,0:T(8,128)S(1)}, u32[]{:S(2)}, u32[]{:S(2)}) collective-permute-start(f32[64,512]{1,0:T(8,128)S(1)} %get-tuple-element.107), channel_id=1, source_target_pairs={{0,120},{8,16},{16,8},{24,32},{32,24},{40,48},{48,40},{56,64},{64,... | collective-permute-start | bytes 393224 | tf_op jit(solution)/shard_map/ppermute | solution.py:327
  37.8 0.5 shard_map.68
  38.3 0.8 %collective-permute-start.15 = (f32[16,512]{1,0:T(8,128)S(1)}, f32[16,512]{1,0:T(8,128)S(1)}, u32[]{:S(2)}, u32[]{:S(2)}) collective-permute-start(f32[16,512]{1,0:T(8,128)S(1)} %get-tuple-element.103), channel_id=1, source_target_pairs={{0,2},{2,0},{4,6},{6,4},{1,3},{3,1},{5,7},{7,5},{8,10},{10,8},{12,... | collective-permute-start | bytes 98312 | tf_op jit(solution)/shard_map/ppermute | solution.py:333
  39.1 1.5 %collective-permute-start.16 = (f32[16,512]{1,0:T(8,128)S(1)}, f32[16,512]{1,0:T(8,128)S(1)}, u32[]{:S(2)}, u32[]{:S(2)}) collective-permute-start(f32[16,512]{1,0:T(8,128)S(1)} %get-tuple-element.104), channel_id=1, source_target_pairs={{0,6},{2,4},{4,2},{6,0},{1,7},{3,5},{5,3},{7,1},{8,14},{10,12},{12... | collective-permute-start | bytes 98312 | tf_op jit(solution)/shard_map/ppermute | solution.py:331
  40.6 0.7 %collective-permute-start.17 = (f32[8,128]{1,0:T(8,128)S(1)}, f32[8,128]{1,0:T(8,128)S(1)}, u32[]{:S(2)}, u32[]{:S(2)}) collective-permute-start(f32[8,128]{1,0:T(8,128)S(1)} %get-tuple-element.105), channel_id=1, source_target_pairs={{0,1},{1,0},{2,3},{3,2},{4,5},{5,4},{6,7},{7,6},{8,9},{9,8},{10,11... | collective-permute-start | bytes 12296 | tf_op jit(solution)/shard_map/ppermute | solution.py:332
  41.3 2.0 %shard_map.69 = (f32[16,64,512]{2,1,0:T(8,128)S(1)}, f32[16,64,512]{2,1,0:T(8,128)S(1)}, f32[16,64,512]{2,1,0:T(8,128)S(1)}) custom-call(f32[16,64,512]{2,1,0:T(8,128)S(1)} %get-tuple-element.108.d_ref, f32[16,64,512]{2,1,0:T(8,128)S(1)} %get-tuple-element.109.r_ref, f32[16,64,512]{2,1,0:T(8,128)S(1)} %get-tuple-element.110.s_ref, ...), custom_call_target="tpu_custom_call" | custom-call | flops 100000000 | tf_op jit(solution)/shard_map/pallas_call | solution.py:46
  43.3 0.1 collective-permute-done.17.refs_4_.refs_2_
  43.4 0.5 collective-permute-done.16.refs_3_.refs_1_
  43.9 0.2 shard_map.70
  44.1 0.1 collective-permute-start.20
  44.2 2.7 %collective-permute-start.21 = (f32[64,512]{1,0:T(8,128)S(1)}, f32[64,512]{1,0:T(8,128)S(1)}, u32[]{:S(2)}, u32[]{:S(2)}) collective-permute-start(f32[64,512]{1,0:T(8,128)S(1)} %get-tuple-element.120), channel_id=1, source_target_pairs={{0,120},{8,16},{16,8},{24,32},{32,24},{40,48},{48,40},{56,64},{64,... | collective-permute-start | bytes 393224 | tf_op jit(solution)/shard_map/ppermute | solution.py:327
  46.9 0.6 shard_map.71
  47.5 0.8 %collective-permute-start.22 = (f32[16,512]{1,0:T(8,128)S(1)}, f32[16,512]{1,0:T(8,128)S(1)}, u32[]{:S(2)}, u32[]{:S(2)}) collective-permute-start(f32[16,512]{1,0:T(8,128)S(1)} %get-tuple-element.121), channel_id=1, source_target_pairs={{0,2},{2,0},{4,6},{6,4},{1,3},{3,1},{5,7},{7,5},{8,10},{10,8},{12,... | collective-permute-start | bytes 98312 | tf_op jit(solution)/shard_map/ppermute | solution.py:333
  48.3 1.7 %collective-permute-start.23 = (f32[16,512]{1,0:T(8,128)S(1)}, f32[16,512]{1,0:T(8,128)S(1)}, u32[]{:S(2)}, u32[]{:S(2)}) collective-permute-start(f32[16,512]{1,0:T(8,128)S(1)} %get-tuple-element.122), channel_id=1, source_target_pairs={{0,6},{2,4},{4,2},{6,0},{1,7},{3,5},{5,3},{7,1},{8,14},{10,12},{12... | collective-permute-start | bytes 98312 | tf_op jit(solution)/shard_map/ppermute | solution.py:331
  50.0 0.7 %collective-permute-start.24 = (f32[8,128]{1,0:T(8,128)S(1)}, f32[8,128]{1,0:T(8,128)S(1)}, u32[]{:S(2)}, u32[]{:S(2)}) collective-permute-start(f32[8,128]{1,0:T(8,128)S(1)} %get-tuple-element.123), channel_id=1, source_target_pairs={{0,1},{1,0},{2,3},{3,2},{4,5},{5,4},{6,7},{7,6},{8,9},{9,8},{10,11... | collective-permute-start | bytes 12296 | tf_op jit(solution)/shard_map/ppermute | solution.py:332
  50.7 1.6 %shard_map.72 = (f32[16,64,512]{2,1,0:T(8,128)S(1)}, f32[16,64,512]{2,1,0:T(8,128)S(1)}) custom-call(f32[16,64,512]{2,1,0:T(8,128)S(1)} %get-tuple-element.115.d_ref, f32[16,64,512]{2,1,0:T(8,128)S(1)} %get-tuple-element.116.r_ref, f32[16,64,512]{2,1,0:T(8,128)S(1)} %get-tuple-element.117.s_ref, f32[16,64,512]{2,1,0:T(8,128)S(1)} %get-tuple-element.86.diag_ref, ...), custom_call_target="tpu_custom_call" | custom-call | flops 100000000 | tf_op jit(solution)/shard_map/pallas_call | solution.py:46
  52.4 0.0 copy-start.3
  52.4 0.4 collective-permute-done.24.refs_4_
  52.8 0.3 collective-permute-done.23.refs_3_
  53.1 1.3 %shard_map.74 = (f32[16,64,512]{2,1,0:T(8,128)S(1)}, f32[128,128]{1,0:T(8,128)}) custom-call(f32[64,512]{1,0:T(8,128)S(1)} %collective-permute-done.20.refs_0_, f32[64,512]{1,0:T(8,128)S(1)} %collective-permute-done.21.refs_1_, f32[16,512]{1,0:T(8,128)S(1)} %collective-permute-done.22.refs_2_, ...), custom_call_target="tpu_custom_call", output_to_operand_aliasing={{0}: (10, {})} | custom-call | tf_op jit(solution)/shard_map/pallas_call | solution.py:46
  54.4 5.6 %all-to-all-start = ((f32[128,1,128]{2,1,0:T(1,128)}), f32[128,1,128]{2,1,0:T(1,128)S(1)}, u32[]{:S(2)}, u32[]{:S(2)}) async-start(f32[128,1,128]{2,1,0:T(1,128)} %bitcast.1), calls=%async_computation | async-start | bytes 131072 | tf_op jit(solution)/shard_map/all_to_all | solution.py:399
  60.0 0.0 copy-start.4
  60.0 1.6 %copy-done.4 = f32[16,64,512]{2,1,0:T(8,128)S(1)} copy-done((f32[16,64,512]{2,1,0:T(8,128)S(1)}, f32[16,64,512]{2,1,0:T(8,128)}, u32[]{:S(2)}) %copy-start.4) | copy-done | bytes 2097176
  61.6 1.3 %shard_map.73 = f32[16,64,512]{2,1,0:T(8,128)} custom-call(f32[16,64,512]{2,1,0:T(8,128)S(1)} %copy-done.4), custom_call_target="tpu_custom_call" | custom-call | flops 100000000 | tf_op jit(solution)/shard_map/pallas_call | solution.py:46
  62.9 1.3 %copy.41 = f32[16,64,512]{2,1,0:T(8,128)} copy(f32[16,64,512]{2,1,0:T(8,128)S(1)} %get-tuple-element.128) | data formatting | bytes 4194304
  64.2 5.2 %all-to-all-done = f32[128,1,128]{2,1,0:T(1,128)S(1)} async-done(((f32[128,1,128]{2,1,0:T(1,128)}), f32[128,1,128]{2,1,0:T(1,128)S(1)}, u32[]{:S(2)}, u32[]{:S(2)}) %all-to-all-start) | async-done | bytes 65568 | tf_op jit(solution)/shard_map/all_to_all | solution.py:399
  69.4 0.1 shard_map.75
  69.5 0.5 copy-done.5
  (19 shorter events, 0.0 us)
Async XLA Ops:
  0.6 7.5 %copy-start.1 = (f32[16,64,512]{2,1,0:T(8,128)S(1)}, f32[16,64,512]{2,1,0:T(8,128)}, u32[]{:S(2)}) copy-start(f32[16,64,512]{2,1,0:T(8,128)} %s_ref.1) | copy-start | bytes 6291460
  0.6 13.3 %copy-start = (f32[3,16,64,512]{3,2,1,0:T(8,128)S(1)}, f32[3,16,64,512]{3,2,1,0:T(8,128)}, u32[]{:S(2)}) copy-start(f32[3,16,64,512]{3,2,1,0:T(8,128)} %velocity_ref.9) | copy-start | bytes 18874372
  1.8 12.2 %copy-start.2 = (f32[16,64,512]{2,1,0:T(8,128)S(1)}, f32[16,64,512]{2,1,0:T(8,128)}, u32[]{:S(2)}) copy-start(f32[16,64,512]{2,1,0:T(8,128)} %reaction_ref.1) | copy-start | bytes 6291460
  1.8 14.4 %collective-permute-start.3 = (f32[64,512]{1,0:T(8,128)S(1)}, f32[64,512]{1,0:T(8,128)S(1)}, u32[]{:S(2)}, u32[]{:S(2)}) collective-permute-start(f32[64,512]{1,0:T(8,128)S(1)} %get-tuple-element.71), channel_id=1, source_target_pairs={{0,8},{8,0},{16,24},{24,16},{32,40},{40,32},{48,56},{56,48},{64,72... | collective-permute-start | bytes 393224 | tf_op jit(solution)/shard_map/ppermute | solution.py:328
  4.0 12.2 %collective-permute-start.4 = (f32[64,512]{1,0:T(8,128)S(1)}, f32[64,512]{1,0:T(8,128)S(1)}, u32[]{:S(2)}, u32[]{:S(2)}) collective-permute-start(f32[64,512]{1,0:T(8,128)S(1)} %get-tuple-element.72), channel_id=1, source_target_pairs={{0,120},{8,16},{16,8},{24,32},{32,24},{40,48},{48,40},{56,64},{64,... | collective-permute-start | bytes 393224 | tf_op jit(solution)/shard_map/ppermute | solution.py:327
  8.3 7.9 %collective-permute-start = (f32[16,512]{1,0:T(8,128)S(1)}, f32[16,512]{1,0:T(8,128)S(1)}, u32[]{:S(2)}, u32[]{:S(2)}) collective-permute-start(f32[16,512]{1,0:T(8,128)S(1)} %get-tuple-element.65), channel_id=1, source_target_pairs={{0,2},{2,0},{4,6},{6,4},{1,3},{3,1},{5,7},{7,5},{8,10},{10,8},{12,... | collective-permute-start | bytes 98312 | tf_op jit(solution)/shard_map/ppermute | solution.py:333
  9.7 6.6 %collective-permute-start.1 = (f32[16,512]{1,0:T(8,128)S(1)}, f32[16,512]{1,0:T(8,128)S(1)}, u32[]{:S(2)}, u32[]{:S(2)}) collective-permute-start(f32[16,512]{1,0:T(8,128)S(1)} %get-tuple-element.66), channel_id=1, source_target_pairs={{0,6},{2,4},{4,2},{6,0},{1,7},{3,5},{5,3},{7,1},{8,14},{10,12},{12... | collective-permute-start | bytes 98312 | tf_op jit(solution)/shard_map/ppermute | solution.py:331
  13.2 3.0 %collective-permute-start.2 = (f32[8,128]{1,0:T(8,128)S(1)}, f32[8,128]{1,0:T(8,128)S(1)}, u32[]{:S(2)}, u32[]{:S(2)}) collective-permute-start(f32[8,128]{1,0:T(8,128)S(1)} %get-tuple-element.67), channel_id=1, source_target_pairs={{0,1},{1,0},{2,3},{3,2},{4,5},{5,4},{6,7},{7,6},{8,9},{9,8},{10,11... | collective-permute-start | bytes 12296 | tf_op jit(solution)/shard_map/ppermute | solution.py:332
  16.4 8.6 %collective-permute-start.8 = (f32[64,512]{1,0:T(8,128)S(1)}, f32[64,512]{1,0:T(8,128)S(1)}, u32[]{:S(2)}, u32[]{:S(2)}) collective-permute-start(f32[64,512]{1,0:T(8,128)S(1)} %get-tuple-element.82), channel_id=1, source_target_pairs={{0,8},{8,0},{16,24},{24,16},{32,40},{40,32},{48,56},{56,48},{64,72... | collective-permute-start | bytes 393224 | tf_op jit(solution)/shard_map/ppermute | solution.py:328
  16.5 8.5 %collective-permute-start.9 = (f32[64,512]{1,0:T(8,128)S(1)}, f32[64,512]{1,0:T(8,128)S(1)}, u32[]{:S(2)}, u32[]{:S(2)}) collective-permute-start(f32[64,512]{1,0:T(8,128)S(1)} %get-tuple-element.83), channel_id=1, source_target_pairs={{0,120},{8,16},{16,8},{24,32},{32,24},{40,48},{48,40},{56,64},{64,... | collective-permute-start | bytes 393224 | tf_op jit(solution)/shard_map/ppermute | solution.py:327
  17.9 7.2 %collective-permute-start.5 = (f32[16,512]{1,0:T(8,128)S(1)}, f32[16,512]{1,0:T(8,128)S(1)}, u32[]{:S(2)}, u32[]{:S(2)}) collective-permute-start(f32[16,512]{1,0:T(8,128)S(1)} %get-tuple-element.79), channel_id=1, source_target_pairs={{0,2},{2,0},{4,6},{6,4},{1,3},{3,1},{5,7},{7,5},{8,10},{10,8},{12,... | collective-permute-start | bytes 98312 | tf_op jit(solution)/shard_map/ppermute | solution.py:333
  19.5 5.5 %collective-permute-start.6 = (f32[16,512]{1,0:T(8,128)S(1)}, f32[16,512]{1,0:T(8,128)S(1)}, u32[]{:S(2)}, u32[]{:S(2)}) collective-permute-start(f32[16,512]{1,0:T(8,128)S(1)} %get-tuple-element.80), channel_id=1, source_target_pairs={{0,6},{2,4},{4,2},{6,0},{1,7},{3,5},{5,3},{7,1},{8,14},{10,12},{12... | collective-permute-start | bytes 98312 | tf_op jit(solution)/shard_map/ppermute | solution.py:331
  22.2 2.8 %collective-permute-start.7 = (f32[8,128]{1,0:T(8,128)S(1)}, f32[8,128]{1,0:T(8,128)S(1)}, u32[]{:S(2)}, u32[]{:S(2)}) collective-permute-start(f32[8,128]{1,0:T(8,128)S(1)} %get-tuple-element.81), channel_id=1, source_target_pairs={{0,1},{1,0},{2,3},{3,2},{4,5},{5,4},{6,7},{7,6},{8,9},{9,8},{10,11... | collective-permute-start | bytes 12296 | tf_op jit(solution)/shard_map/ppermute | solution.py:332
  25.2 9.3 %collective-permute-start.13 = (f32[64,512]{1,0:T(8,128)S(1)}, f32[64,512]{1,0:T(8,128)S(1)}, u32[]{:S(2)}, u32[]{:S(2)}) collective-permute-start(f32[64,512]{1,0:T(8,128)S(1)} %get-tuple-element.94), channel_id=1, source_target_pairs={{0,8},{8,0},{16,24},{24,16},{32,40},{40,32},{48,56},{56,48},{64,72... | collective-permute-start | bytes 393224 | tf_op jit(solution)/shard_map/ppermute | solution.py:328
  25.3 9.2 %collective-permute-start.14 = (f32[64,512]{1,0:T(8,128)S(1)}, f32[64,512]{1,0:T(8,128)S(1)}, u32[]{:S(2)}, u32[]{:S(2)}) collective-permute-start(f32[64,512]{1,0:T(8,128)S(1)} %get-tuple-element.95), channel_id=1, source_target_pairs={{0,120},{8,16},{16,8},{24,32},{32,24},{40,48},{48,40},{56,64},{64,... | collective-permute-start | bytes 393224 | tf_op jit(solution)/shard_map/ppermute | solution.py:327
  29.1 5.3 %collective-permute-start.10 = (f32[16,512]{1,0:T(8,128)S(1)}, f32[16,512]{1,0:T(8,128)S(1)}, u32[]{:S(2)}, u32[]{:S(2)}) collective-permute-start(f32[16,512]{1,0:T(8,128)S(1)} %get-tuple-element.91), channel_id=1, source_target_pairs={{0,2},{2,0},{4,6},{6,4},{1,3},{3,1},{5,7},{7,5},{8,10},{10,8},{12,... | collective-permute-start | bytes 98312 | tf_op jit(solution)/shard_map/ppermute | solution.py:333
  29.6 4.9 %collective-permute-start.11 = (f32[16,512]{1,0:T(8,128)S(1)}, f32[16,512]{1,0:T(8,128)S(1)}, u32[]{:S(2)}, u32[]{:S(2)}) collective-permute-start(f32[16,512]{1,0:T(8,128)S(1)} %get-tuple-element.92), channel_id=1, source_target_pairs={{0,6},{2,4},{4,2},{6,0},{1,7},{3,5},{5,3},{7,1},{8,14},{10,12},{12... | collective-permute-start | bytes 98312 | tf_op jit(solution)/shard_map/ppermute | solution.py:331
  31.6 2.8 %collective-permute-start.12 = (f32[8,128]{1,0:T(8,128)S(1)}, f32[8,128]{1,0:T(8,128)S(1)}, u32[]{:S(2)}, u32[]{:S(2)}) collective-permute-start(f32[8,128]{1,0:T(8,128)S(1)} %get-tuple-element.93), channel_id=1, source_target_pairs={{0,1},{1,0},{2,3},{3,2},{4,5},{5,4},{6,7},{7,6},{8,9},{9,8},{10,11... | collective-permute-start | bytes 12296 | tf_op jit(solution)/shard_map/ppermute | solution.py:332
  34.7 9.2 %collective-permute-start.18 = (f32[64,512]{1,0:T(8,128)S(1)}, f32[64,512]{1,0:T(8,128)S(1)}, u32[]{:S(2)}, u32[]{:S(2)}) collective-permute-start(f32[64,512]{1,0:T(8,128)S(1)} %get-tuple-element.106), channel_id=1, source_target_pairs={{0,8},{8,0},{16,24},{24,16},{32,40},{40,32},{48,56},{56,48},{64,72... | collective-permute-start | bytes 393224 | tf_op jit(solution)/shard_map/ppermute | solution.py:328
  34.8 9.1 %collective-permute-start.19 = (f32[64,512]{1,0:T(8,128)S(1)}, f32[64,512]{1,0:T(8,128)S(1)}, u32[]{:S(2)}, u32[]{:S(2)}) collective-permute-start(f32[64,512]{1,0:T(8,128)S(1)} %get-tuple-element.107), channel_id=1, source_target_pairs={{0,120},{8,16},{16,8},{24,32},{32,24},{40,48},{48,40},{56,64},{64,... | collective-permute-start | bytes 393224 | tf_op jit(solution)/shard_map/ppermute | solution.py:327
  38.3 5.1 %collective-permute-start.15 = (f32[16,512]{1,0:T(8,128)S(1)}, f32[16,512]{1,0:T(8,128)S(1)}, u32[]{:S(2)}, u32[]{:S(2)}) collective-permute-start(f32[16,512]{1,0:T(8,128)S(1)} %get-tuple-element.103), channel_id=1, source_target_pairs={{0,2},{2,0},{4,6},{6,4},{1,3},{3,1},{5,7},{7,5},{8,10},{10,8},{12,... | collective-permute-start | bytes 98312 | tf_op jit(solution)/shard_map/ppermute | solution.py:333
  39.1 4.9 %collective-permute-start.16 = (f32[16,512]{1,0:T(8,128)S(1)}, f32[16,512]{1,0:T(8,128)S(1)}, u32[]{:S(2)}, u32[]{:S(2)}) collective-permute-start(f32[16,512]{1,0:T(8,128)S(1)} %get-tuple-element.104), channel_id=1, source_target_pairs={{0,6},{2,4},{4,2},{6,0},{1,7},{3,5},{5,3},{7,1},{8,14},{10,12},{12... | collective-permute-start | bytes 98312 | tf_op jit(solution)/shard_map/ppermute | solution.py:331
  40.6 2.8 %collective-permute-start.17 = (f32[8,128]{1,0:T(8,128)S(1)}, f32[8,128]{1,0:T(8,128)S(1)}, u32[]{:S(2)}, u32[]{:S(2)}) collective-permute-start(f32[8,128]{1,0:T(8,128)S(1)} %get-tuple-element.105), channel_id=1, source_target_pairs={{0,1},{1,0},{2,3},{3,2},{4,5},{5,4},{6,7},{7,6},{8,9},{9,8},{10,11... | collective-permute-start | bytes 12296 | tf_op jit(solution)/shard_map/ppermute | solution.py:332
  44.1 9.0 %collective-permute-start.20 = (f32[64,512]{1,0:T(8,128)S(1)}, f32[64,512]{1,0:T(8,128)S(1)}, u32[]{:S(2)}, u32[]{:S(2)}) collective-permute-start(f32[64,512]{1,0:T(8,128)S(1)} %get-tuple-element.119), channel_id=1, source_target_pairs={{0,8},{8,0},{16,24},{24,16},{32,40},{40,32},{48,56},{56,48},{64,72... | collective-permute-start | bytes 393224 | tf_op jit(solution)/shard_map/ppermute | solution.py:328
  44.2 8.9 %collective-permute-start.21 = (f32[64,512]{1,0:T(8,128)S(1)}, f32[64,512]{1,0:T(8,128)S(1)}, u32[]{:S(2)}, u32[]{:S(2)}) collective-permute-start(f32[64,512]{1,0:T(8,128)S(1)} %get-tuple-element.120), channel_id=1, source_target_pairs={{0,120},{8,16},{16,8},{24,32},{32,24},{40,48},{48,40},{56,64},{64,... | collective-permute-start | bytes 393224 | tf_op jit(solution)/shard_map/ppermute | solution.py:327
  47.5 5.3 %collective-permute-start.22 = (f32[16,512]{1,0:T(8,128)S(1)}, f32[16,512]{1,0:T(8,128)S(1)}, u32[]{:S(2)}, u32[]{:S(2)}) collective-permute-start(f32[16,512]{1,0:T(8,128)S(1)} %get-tuple-element.121), channel_id=1, source_target_pairs={{0,2},{2,0},{4,6},{6,4},{1,3},{3,1},{5,7},{7,5},{8,10},{10,8},{12,... | collective-permute-start | bytes 98312 | tf_op jit(solution)/shard_map/ppermute | solution.py:333
  48.3 4.9 %collective-permute-start.23 = (f32[16,512]{1,0:T(8,128)S(1)}, f32[16,512]{1,0:T(8,128)S(1)}, u32[]{:S(2)}, u32[]{:S(2)}) collective-permute-start(f32[16,512]{1,0:T(8,128)S(1)} %get-tuple-element.122), channel_id=1, source_target_pairs={{0,6},{2,4},{4,2},{6,0},{1,7},{3,5},{5,3},{7,1},{8,14},{10,12},{12... | collective-permute-start | bytes 98312 | tf_op jit(solution)/shard_map/ppermute | solution.py:331
  50.0 2.8 %collective-permute-start.24 = (f32[8,128]{1,0:T(8,128)S(1)}, f32[8,128]{1,0:T(8,128)S(1)}, u32[]{:S(2)}, u32[]{:S(2)}) collective-permute-start(f32[8,128]{1,0:T(8,128)S(1)} %get-tuple-element.123), channel_id=1, source_target_pairs={{0,1},{1,0},{2,3},{3,2},{4,5},{5,4},{6,7},{7,6},{8,9},{9,8},{10,11... | collective-permute-start | bytes 12296 | tf_op jit(solution)/shard_map/ppermute | solution.py:332
  52.4 2.0 %copy-start.3 = (f32[16,64,512]{2,1,0:T(8,128)}, f32[16,64,512]{2,1,0:T(8,128)S(1)}, u32[]{:S(2)}) copy-start(f32[16,64,512]{2,1,0:T(8,128)S(1)} %get-tuple-element.118.held_ref) | copy-start | bytes 6291460
  54.4 15.0 %all-to-all-start = ((f32[128,1,128]{2,1,0:T(1,128)}), f32[128,1,128]{2,1,0:T(1,128)S(1)}, u32[]{:S(2)}, u32[]{:S(2)}) async-start(f32[128,1,128]{2,1,0:T(1,128)} %bitcast.1), calls=%async_computation | async-start | bytes 131072 | tf_op jit(solution)/shard_map/all_to_all | solution.py:399
  60.0 1.6 %copy-start.4 = (f32[16,64,512]{2,1,0:T(8,128)S(1)}, f32[16,64,512]{2,1,0:T(8,128)}, u32[]{:S(2)}) copy-start(f32[16,64,512]{2,1,0:T(8,128)} %copy-done.3) | copy-start | bytes 6291460
  69.5 0.5 copy-start.5
